TPU v7x, 32 devices: a whole 2x2x4 slice. The times are simulated.
32 devices in a mesh: section: 4 (over x, core), expert: 2 (over y), dp: 4 (over z).
Axes of the slice: x: 2, y: 2, z: 4, core: 2. Of those that a mesh axis runs over, the one named last changes fastest.
Arguments:
- fwd_input: bfloat16 [4, 256, 2048], P('section', 'dp', 'expert'), may hold values from -6 to 6
- fresh_input: bfloat16 [1, 256, 2048], P(None, 'dp', 'expert'), may hold values from -6 to 6
- fwd_experts: int32 [4, 2, 256, 2], P('section', None, 'dp'), may hold values from 0 to 3, all different within a row; in each aligned block of 64 rows (0 to 63, 64 to 127, ..., all dimensions but the last counted through in order) at most 36 rows name the same one
- fwd_gates: float32 [4, 2, 256, 2], P('section', None, 'dp'), may hold values from 0.2 to 1
- bwd_saved: bfloat16 [4, 2, 256, 2048], P('section', None, 'dp', 'expert'), may hold values from -6 to 6
- bwd_experts: int32 [4, 2, 256, 2], P('section', None, 'dp'), may hold values from 0 to 3, all different within a row; in each aligned block of 64 rows (0 to 63, 64 to 127, ..., all dimensions but the last counted through in order) at most 36 rows name the same one
- bwd_gates: float32 [4, 2, 256, 2], P('section', None, 'dp'), may hold values from 0.2 to 1
- out_grad: bfloat16 [4, 256, 2048], P('section', 'dp', 'expert'), may hold values from -6 to 6
- fresh_grad: bfloat16 [1, 256, 2048], P(None, 'dp', 'expert'), may hold values from -6 to 6
- gate_proj: bfloat16 [4, 4, 7168, 2048], P('section', 'dp', 'expert'), may hold values from -0.125 to 0.125
- down_proj: bfloat16 [4, 4, 7168, 2048], P('section', 'dp', 'expert'), may hold values from -0.0625 to 0.0625
Outputs:
- fwd_output: bfloat16 [4, 2, 256, 2048], P('section', None, 'dp', 'expert')
- input_grad: bfloat16 [4, 2, 256, 2048], P('section', None, 'dp', 'expert')
- gate_grad: bfloat16 [4, 4, 7168, 2048], P('section', 'dp', 'expert')
- down_grad: bfloat16 [4, 4, 7168, 2048], P('section', 'dp', 'expert')
Inputs may be any that keep to these rules, and one draw needn't show every extreme that they name: `fwd_experts`: each token names two different experts. In every aligned block of 64 tokens (one index of dp, one section and step) no expert is named more than 36 times, and in some blocks one expert is named exactly 36 times. `bwd_experts`: each token names two different experts. In every aligned block of 64 tokens (one index of dp, one section and step) no expert is named more than 36 times, and in some blocks one expert is named exactly 36 times.
All inputs are finite; a program needn't handle non-finite values.
Results may differ from a plain program's by a relative error of at most 0.0062.
Values may be sent and summed in bfloat16 or wider, within the bound.
A program may use at most 256 MiB of HBM per device.

v0:
```python
import math

import jax
import jax.numpy as jnp
from jax import lax
from jax.sharding import PartitionSpec as P

D = 2048
FF = 7168
EXPERTS = 4
CAP = 36


precise = lax.Precision.HIGHEST


def shifted(value, axis, steps):
    count = lax.axis_size(axis)
    initial, last = (max(0, -steps), min(count, count - steps))
    return lax.ppermute(value, axis, [(source, source + steps) for source in range(initial, last)])


def slot_plan(experts, number, capacity):
    flattened = experts.reshape(-1)
    assigned = flattened.shape[0]
    one_hot = (flattened[:, None] == jnp.arange(number, dtype=jnp.int32)[None, :]).astype(
        jnp.float32
    )
    earlier = (jnp.arange(assigned)[:, None] > jnp.arange(assigned)[None, :]).astype(jnp.float32)
    prior_count = jnp.dot(earlier, one_hot, precision=precise)
    position = jnp.sum(prior_count * one_hot, axis=1).astype(jnp.int32)
    target = flattened * capacity + position
    matches = jnp.arange(number * capacity, dtype=jnp.int32)[:, None] == target[None, :]
    source = jnp.sum(jnp.where(matches, jnp.arange(assigned, dtype=jnp.int32)[None, :], 0), axis=1)
    filled = jnp.any(matches, axis=1)
    return (target, source, filled)


def fill_rows(values, source, filled, number, capacity):
    rows = jnp.take(values, source // 2, axis=0)
    rows = jnp.where(filled[:, None], rows, jnp.zeros((), values.dtype))
    return rows.reshape(number, capacity, values.shape[-1])


def collect(partial_out):
    number, capacity, columns = partial_out.shape
    homed = lax.all_to_all(partial_out, "dp", split_axis=0, concat_axis=0, tiled=True)
    pieces = lax.all_to_all(
        homed.reshape(1, number, capacity, columns),
        "expert",
        split_axis=3,
        concat_axis=0,
        tiled=True,
    )
    return jnp.sum(pieces.astype(jnp.float32), axis=0)


def combine(returned, target, base, gate_values):
    number, capacity, columns = returned.shape
    picked = jnp.take(returned.reshape(number * capacity, columns), target, axis=0)
    picked = picked.reshape(base.shape[0], 2, columns)
    if gate_values is None:
        weighted = jnp.sum(picked, axis=1)
    else:
        weighted = jnp.sum(gate_values[:, :, None] * picked, axis=1)
    return (base.astype(jnp.float32) + weighted).astype(jnp.bfloat16)


def forward_layer(whole, part, experts, gate_values, gate_weight, down_weight):
    columns = whole.shape[-1]
    target, source, filled = slot_plan(experts, EXPERTS, CAP)
    slot_buffer = fill_rows(whole, source, filled, EXPERTS, CAP)
    arrived = lax.all_to_all(slot_buffer, "dp", split_axis=0, concat_axis=0, tiled=True)
    flat_rows = arrived.reshape(-1, columns)
    before_act = jnp.einsum("rd,fd->rf", flat_rows, gate_weight, preferred_element_type=jnp.float32)
    hidden = jax.nn.silu(before_act).astype(jnp.bfloat16)
    partial_out = jnp.dot(hidden, down_weight, preferred_element_type=jnp.float32).astype(
        jnp.bfloat16
    )
    returned = collect(partial_out.reshape(arrived.shape))
    return combine(returned, target, part, gate_values)


def backward_layer(stored, experts, gate_values, whole_grad, part_grad, gate_weight, down_weight):
    columns = stored.shape[-1]
    target, source, filled = slot_plan(experts, EXPERTS, CAP)
    input_slots = fill_rows(stored, source, filled, EXPERTS, CAP)
    slot_gate = jnp.take(gate_values.reshape(-1), source)
    grad_rows = jnp.take(whole_grad, source // 2, axis=0).astype(jnp.float32) * slot_gate[:, None]
    grad_rows = jnp.where(filled[:, None], grad_rows, jnp.float32(0.0)).astype(jnp.bfloat16)
    grad_slots = grad_rows.reshape(EXPERTS, CAP, columns)
    input_rows, scaled_rows = (
        lax.all_to_all(input_slots, "dp", split_axis=0, concat_axis=0, tiled=True),
        lax.all_to_all(grad_slots, "dp", split_axis=0, concat_axis=0, tiled=True),
    )
    flat_in = input_rows.reshape(-1, columns)
    flat_grad = scaled_rows.reshape(-1, columns)
    before_act = jnp.einsum("rd,fd->rf", flat_in, gate_weight, preferred_element_type=jnp.float32)
    hidden = jax.nn.silu(before_act).astype(jnp.bfloat16)
    down_step = jnp.einsum("rf,rd->fd", hidden, flat_grad, preferred_element_type=jnp.float32)
    through = jnp.einsum("rd,fd->rf", flat_grad, down_weight, preferred_element_type=jnp.float32)
    sigmoid = jax.nn.sigmoid(before_act)
    slope_grad = (through * sigmoid * (1.0 + before_act * (1.0 - sigmoid))).astype(jnp.bfloat16)
    gate_step = jnp.einsum("rf,rd->fd", slope_grad, flat_in, preferred_element_type=jnp.float32)
    partial_out = jnp.dot(slope_grad, gate_weight, preferred_element_type=jnp.float32).astype(
        jnp.bfloat16
    )
    returned = collect(partial_out.reshape(input_rows.shape))
    return (combine(returned, target, part_grad, None), gate_step, down_step)


def on_device(
    fwd_input,
    fresh_input,
    fwd_experts,
    fwd_gates,
    bwd_saved,
    bwd_experts,
    bwd_gates,
    out_grad,
    fresh_grad,
    gate_proj,
    down_proj,
):
    gate_weight = gate_proj[0, 0]
    down_weight = down_proj[0, 0]
    section_count = lax.axis_size("section")
    section_index = lax.axis_index("section")
    is_first = section_index == 0
    is_last = section_index == section_count - 1
    tick_count = fwd_experts.shape[1]
    saved_full = lax.all_gather(bwd_saved[0], "expert", axis=2, tiled=True)
    input_part = fwd_input[0]
    grad_part = out_grad[0]
    gate_total = jnp.zeros(gate_weight.shape, jnp.float32)
    down_total = jnp.zeros(down_weight.shape, jnp.float32)
    squares = jnp.zeros((), jnp.float32)
    forward_list = []
    backward_list = []
    for tick_index in range(tick_count):
        input_full, grad_full = (
            lax.all_gather(input_part, "expert", axis=1, tiled=True),
            lax.all_gather(grad_part, "expert", axis=1, tiled=True),
        )
        produced = forward_layer(
            input_full,
            input_part,
            fwd_experts[0, tick_index],
            fwd_gates[0, tick_index],
            gate_weight,
            down_weight,
        )
        returned_grad, gate_step, down_step = backward_layer(
            saved_full[tick_index],
            bwd_experts[0, tick_index],
            bwd_gates[0, tick_index],
            grad_full,
            grad_part,
            gate_weight,
            down_weight,
        )
        forward_list.append(produced)
        backward_list.append(returned_grad)
        growth = (
            2.0 * jnp.sum(gate_total * gate_step)
            + jnp.sum(gate_step * gate_step)
            + 2.0 * jnp.sum(down_total * down_step)
            + jnp.sum(down_step * down_step)
        )
        squares = squares + lax.psum(growth, ("section", "expert", "dp"))
        gate_total = gate_total + gate_step
        down_total = down_total + down_step
        if tick_index + 1 < tick_count:
            arriving = shifted(produced, "section", 1)
            input_part = jnp.where(is_first, fresh_input[tick_index], arriving)
            leaving = shifted(returned_grad, "section", -1)
            grad_part = jnp.where(is_last, fresh_grad[tick_index], leaving)
    clip_limit = 0.25 * math.sqrt(2.0 * section_count * EXPERTS * FF * D)
    factor = clip_limit / jnp.maximum(jnp.sqrt(squares), clip_limit)
    fwd_output = jnp.stack(forward_list)[None]
    input_grad = jnp.stack(backward_list)[None]
    gate_grad = (gate_total * factor).astype(jnp.bfloat16)[None, None]
    down_grad = (down_total * factor).astype(jnp.bfloat16)[None, None]
    return (fwd_output, input_grad, gate_grad, down_grad)


def solution(mesh):
    in_specs = (
        P("section", "dp", "expert"),
        P(None, "dp", "expert"),
        P("section", None, "dp", None),
        P("section", None, "dp", None),
        P("section", None, "dp", "expert"),
        P("section", None, "dp", None),
        P("section", None, "dp", None),
        P("section", "dp", "expert"),
        P(None, "dp", "expert"),
        P("section", "dp", "expert", None),
        P("section", "dp", "expert", None),
    )
    out_specs = (
        P("section", None, "dp", "expert"),
        P("section", None, "dp", "expert"),
        P("section", "dp", "expert", None),
        P("section", "dp", "expert", None),
    )
    return jax.shard_map(
        on_device, mesh=mesh, in_specs=in_specs, out_specs=out_specs, check_vma=False
    )
```

profile of v0, /device:TPU:12, one launch (start us, length us, event | category | flops | bytes accessed | tf_op | source)
XLA Modules:
  0.0 493.5 jit_solution(201202611185256793)
XLA Ops:
  2.5 6.1 %all-gather = bf16[1,64,2048]{2,1,0:T(8,128)(2,1)S(1)} all-gather(bf16[1,64,1024]{2,1,0:T(8,128)(2,1)} %param.17), channel_id=2, replica_groups=mesh['section'=4,'expert'=2,'dp'=4] {'expert'}, dimensions={2}, use_global_device_ids=true | all-gather | bytes 393216 | tf_op jit(solution)/shard_map/all_gather | solution.py:142
  10.8 5.3 %all-to-all-start = ((bf16[4,36,2048]{2,1,0:T(8,128)(2,1)}), bf16[4,36,2048]{2,1,0:T(8,128)(2,1)S(1)}, u32[]{:S(2)}, u32[]{:S(2)}) async-start(bf16[4,36,2048]{2,1,0:T(8,128)(2,1)} %reshape.173), calls=%async_computation | async-start | bytes 1310720 | tf_op jit(solution)/shard_map/all_to_all | solution.py:73
  23.8 5.6 %all-gather.1 = bf16[1,64,2048]{2,1,0:T(8,128)(2,1)S(1)} all-gather(bf16[1,64,1024]{2,1,0:T(8,128)(2,1)S(1)} %copy-done.10), channel_id=3, replica_groups=mesh['section'=4,'expert'=2,'dp'=4] {'expert'}, dimensions={2}, use_global_device_ids=true | all-gather | bytes 393216 | tf_op jit(solution)/shard_map/all_gather | solution.py:143
  31.9 7.0 %all-gather.2 = bf16[1,2,64,2048]{3,2,1,0:T(8,128)(2,1)S(1)} all-gather(bf16[1,2,64,1024]{3,2,1,0:T(8,128)(2,1)S(1)} %copy-done.15), channel_id=4, replica_groups=mesh['section'=4,'expert'=2,'dp'=4] {'expert'}, dimensions={3}, use_global_device_ids=true | all-gather | bytes 786432 | tf_op jit(solution)/shard_map/all_gather | solution.py:132
  46.0 5.1 %all-to-all-start.7 = ((bf16[4,36,2048]{2,1,0:T(8,128)(2,1)}), bf16[4,36,2048]{2,1,0:T(8,128)(2,1)S(1)}, u32[]{:S(2)}, u32[]{:S(2)}) async-start(bf16[4,36,2048]{2,1,0:T(8,128)(2,1)} %reshape.187), calls=%async_computation.7 | async-start | bytes 1310720 | tf_op jit(solution)/shard_map/all_to_all | solution.py:93
  52.5 9.0 %all-to-all-done.7 = bf16[4,36,2048]{2,1,0:T(8,128)(2,1)S(1)} async-done(((bf16[4,36,2048]{2,1,0:T(8,128)(2,1)}), bf16[4,36,2048]{2,1,0:T(8,128)(2,1)S(1)}, u32[]{:S(2)}, u32[]{:S(2)}) %all-to-all-start.7) | async-done | bytes 589856 | tf_op jit(solution)/shard_map/all_to_all | solution.py:93
  61.5 7.3 %all-to-all-start.6 = ((bf16[4,36,2048]{2,1,0:T(8,128)(2,1)}), bf16[4,36,2048]{2,1,0:T(8,128)(2,1)S(1)}, u32[]{:S(2)}, u32[]{:S(2)}) async-start(bf16[4,36,2048]{2,1,0:T(8,128)(2,1)} %reshape.185), calls=%async_computation.6 | async-start | bytes 1310720 | tf_op jit(solution)/shard_map/all_to_all | solution.py:94
  68.7 13.5 %fusion.46 = bf16[144,2048]{1,0:T(8,128)(2,1)S(1)} fusion(bf16[1,1,3584,2048]{3,2,1,0:T(8,128)(2,1)} %param.27, bf16[144,2048]{1,0:T(8,128)(2,1)S(1)} %reshape.174, bf16[1,1,3584,2048]{3,2,1,0:T(8,128)(2,1)} %param.26), kind=kOutput, calls=%fused_computation.52 | convolution fusion | flops 4230733824 | bytes 30539776 | tf_op jit(solution)/shard_map/dot_general | solution.py:77
  83.3 10.4 %fusion.16 = f32[144,3584]{1,0:T(8,128)S(1)} fusion(bf16[144,2048]{1,0:T(8,128)(2,1)S(1)} %reshape.188, bf16[1,1,3584,2048]{3,2,1,0:T(8,128)(2,1)} %param.26), kind=kOutput, calls=%fused_computation.38 | convolution fusion | flops 2113929216 | bytes 17334272 | tf_op jit(solution)/shard_map/rd,fd->rf/dot_general | solution.py:98
  93.7 5.3 %all-to-all-start.11 = ((bf16[4,36,2048]{2,1,0:T(8,128)(2,1)}), bf16[4,36,2048]{2,1,0:T(8,128)(2,1)}, u32[]{:S(2)}, u32[]{:S(2)}) async-start(bf16[4,36,2048]{2,1,0:T(8,128)(2,1)} %reshape.195), calls=%async_computation.11 | async-start | bytes 1310720 | tf_op jit(solution)/shard_map/all_to_all | solution.py:93
  100.0 10.6 %fusion.34 = bf16[144,3584]{1,0:T(8,128)(2,1)S(1)} fusion(bf16[144,2048]{1,0:T(8,128)(2,1)} %reshape.186, bf16[1,1,3584,2048]{3,2,1,0:T(8,128)(2,1)} %param.27, f32[144,3584]{1,0:T(8,128)S(1)} %fusion.16), kind=kOutput, calls=%fused_computation.48 | convolution fusion | flops 2118574080 | bytes 18366464 | tf_op jit(solution)/shard_map/rd,fd->rf/dot_general | solution.py:101
  110.5 8.3 %fusion.40 = bf16[144,2048]{1,0:T(8,128)(2,1)} fusion(bf16[144,3584]{1,0:T(8,128)(2,1)S(1)} %fusion.34, bf16[1,1,3584,2048]{3,2,1,0:T(8,128)(2,1)} %param.26), kind=kOutput, calls=%fused_computation.50 | convolution fusion | flops 2114224128 | bytes 16302080 | tf_op jit(solution)/shard_map/dot_general | solution.py:105
  118.9 2.0 reshape.189
  120.9 5.1 %all-to-all-start.1 = ((bf16[4,36,2048]{2,1,0:T(8,128)(2,1)}), bf16[4,36,2048]{2,1,0:T(8,128)(2,1)}, u32[]{:S(2)}, u32[]{:S(2)}) async-start(bf16[4,36,2048]{2,1,0:T(8,128)(2,1)} %reshape.175), calls=%async_computation.1 | async-start | bytes 1310720 | tf_op jit(solution)/shard_map/all_to_all | solution.py:47
  126.0 2.0 reshape.196
  128.0 12.8 %fusion.60 = f32[3584,2048]{1,0:T(8,128)} fusion(bf16[144,2048]{1,0:T(8,128)(2,1)} %reshape.186, f32[144,3584]{1,0:T(8,128)S(1)} %fusion.16), kind=kOutput, calls=%fused_computation.70 | convolution fusion | flops 2116509696 | bytes 32014336 | tf_op jit(solution)/shard_map/rf,rd->fd/dot_general | solution.py:100
  140.8 5.5 %all-to-all-start.8 = ((bf16[4,36,2048]{2,1,0:T(8,128)(2,1)}), bf16[4,36,2048]{2,1,0:T(8,128)(2,1)}, u32[]{:S(2)}, u32[]{:S(2)}) async-start(bf16[4,36,2048]{2,1,0:T(8,128)(2,1)} %reshape.189), calls=%async_computation.8 | async-start | bytes 1310720 | tf_op jit(solution)/shard_map/all_to_all | solution.py:47
  146.3 12.7 %fusion.91 = f32[3584,2048]{1,0:T(8,128)} fusion(bf16[144,3584]{1,0:T(8,128)(2,1)S(1)} %fusion.34, bf16[144,2048]{1,0:T(8,128)(2,1)} %copy-done), kind=kOutput, calls=%fused_computation.184 | convolution fusion | flops 2113929216 | bytes 30982144 | tf_op jit(solution)/shard_map/rf,rd->fd/dot_general | solution.py:104
  159.0 2.9 copy.77
  161.9 5.7 %reshape.346 = bf16[2,2,73728]{2,1,0:T(2,128)(2,1)} reshape(bf16[2048,1,4,36]{3,2,1,0:T(4,128)(2,1)S(1)} %bitcast.140) | data formatting | bytes 1179648
  167.7 4.0 all-to-all-start.2
  171.7 11.4 %fusion.12 = f32[144,3584]{1,0:T(8,128)} fusion(bf16[144,2048]{1,0:T(8,128)(2,1)S(1)} %copy-done.1, bf16[1,1,3584,2048]{3,2,1,0:T(8,128)(2,1)} %param.26), kind=kOutput, calls=%fused_computation.34 | convolution fusion | flops 2113929216 | bytes 17334272 | tf_op jit(solution)/shard_map/rd,fd->rf/dot_general | solution.py:98
  183.1 2.9 copy.87
  186.0 5.7 %reshape.350 = bf16[2,2,73728]{2,1,0:T(2,128)(2,1)} reshape(bf16[2048,1,4,36]{3,2,1,0:T(4,128)(2,1)S(1)} %bitcast.141) | data formatting | bytes 1179648
  192.6 3.7 all-to-all-start.9
  196.3 6.7 %reshape.347 = bf16[2048,1,4,36]{3,2,1,0:T(4,128)(2,1)S(1)} reshape(bf16[2,2,73728]{2,1,0:T(2,128)(2,1)} %copy-done.3) | data formatting | bytes 1179648
  210.2 1.9 collective-permute-start
  212.2 6.0 %reshape.351 = bf16[2048,1,4,36]{3,2,1,0:T(4,128)(2,1)S(1)} reshape(bf16[2,2,73728]{2,1,0:T(2,128)(2,1)S(1)} %all-to-all-done.9) | data formatting | bytes 1179648
  225.7 5.6 %all_gather.16 = bf16[64,2048]{1,0:T(8,128)(2,1)S(1)} all-gather(bf16[64,1024]{1,0:T(8,128)(2,1)S(1)} %bitcast_select_fusion.1), channel_id=1, replica_groups=mesh['section'=4,'expert'=2,'dp'=4] {'expert'}, dimensions={1}, use_global_device_ids=true | all-gather | bytes 393216 | tf_op jit(solution)/shard_map/all_gather | solution.py:142
  233.5 5.1 %all-to-all-start.3 = ((bf16[4,36,2048]{2,1,0:T(8,128)(2,1)}), bf16[4,36,2048]{2,1,0:T(8,128)(2,1)S(1)}, u32[]{:S(2)}, u32[]{:S(2)}) async-start(bf16[4,36,2048]{2,1,0:T(8,128)(2,1)} %reshape.179), calls=%async_computation.3 | async-start | bytes 1310720 | tf_op jit(solution)/shard_map/all_to_all | solution.py:73
  239.3 6.6 %all_gather.19 = bf16[64,2048]{1,0:T(8,128)(2,1)S(1)} all-gather(bf16[64,1024]{1,0:T(8,128)(2,1)S(1)} %bitcast_select_fusion), channel_id=1, replica_groups=mesh['section'=4,'expert'=2,'dp'=4] {'expert'}, dimensions={1}, use_global_device_ids=true | all-gather | bytes 393216 | tf_op jit(solution)/shard_map/all_gather | solution.py:143
  248.4 4.9 all-to-all-done.3
  253.3 6.7 %all-to-all-start.10 = ((bf16[4,36,2048]{2,1,0:T(8,128)(2,1)}), bf16[4,36,2048]{2,1,0:T(8,128)(2,1)S(1)}, u32[]{:S(2)}, u32[]{:S(2)}) async-start(bf16[4,36,2048]{2,1,0:T(8,128)(2,1)} %reshape.193), calls=%async_computation.10 | async-start | bytes 1310720 | tf_op jit(solution)/shard_map/all_to_all | solution.py:94
  260.2 13.4 %fusion.49 = bf16[144,2048]{1,0:T(8,128)(2,1)S(1)} fusion(bf16[1,1,3584,2048]{3,2,1,0:T(8,128)(2,1)} %param.27, bf16[144,2048]{1,0:T(8,128)(2,1)S(1)} %reshape.180, bf16[1,1,3584,2048]{3,2,1,0:T(8,128)(2,1)} %param.26), kind=kOutput, calls=%fused_computation.53 | convolution fusion | flops 4230733824 | bytes 30539776 | tf_op jit(solution)/shard_map/dot_general | solution.py:77
  275.1 7.1 %all-to-all-start.4 = ((bf16[4,36,2048]{2,1,0:T(8,128)(2,1)}), bf16[4,36,2048]{2,1,0:T(8,128)(2,1)S(1)}, u32[]{:S(2)}, u32[]{:S(2)}) async-start(bf16[4,36,2048]{2,1,0:T(8,128)(2,1)} %reshape.181), calls=%async_computation.4 | async-start | bytes 1310720 | tf_op jit(solution)/shard_map/all_to_all | solution.py:47
  282.3 12.0 %fusion.37 = bf16[144,3584]{1,0:T(8,128)(2,1)} fusion(bf16[144,2048]{1,0:T(8,128)(2,1)S(1)} %reshape.194, bf16[1,1,3584,2048]{3,2,1,0:T(8,128)(2,1)} %param.27, f32[144,3584]{1,0:T(8,128)} %fusion.12), kind=kOutput, calls=%fused_computation.49 | convolution fusion | flops 2118574080 | bytes 18366464 | tf_op jit(solution)/shard_map/rd,fd->rf/dot_general | solution.py:101
  294.3 20.4 %multiply_reduce_fusion = (f32[]{:T(128)}, f32[]{:T(128)}, f32[]{:T(128)}, f32[]{:T(128)}, f32[3584,2048]{1,0:T(8,128)}) fusion(f32[3584,2048]{1,0:T(8,128)} %fusion.60, bf16[144,2048]{1,0:T(8,128)(2,1)S(1)} %reshape.194, f32[144,3584]{1,0:T(8,128)S(1)} %copy-done.6), kind=kOutput, calls=%fused_computation.14 | convolution fusion | flops 2175229952 | bytes 61374480 | tf_op jit(solution)/shard_map/rf,rd->fd/dot_general | solution.py:100
  314.7 7.8 %fusion.43 = bf16[144,2048]{1,0:T(8,128)(2,1)S(1)} fusion(bf16[144,3584]{1,0:T(8,128)(2,1)} %fusion.37, bf16[1,1,3584,2048]{3,2,1,0:T(8,128)(2,1)} %param.26), kind=kOutput, calls=%fused_computation.51 | convolution fusion | flops 2114224128 | bytes 16302080 | tf_op jit(solution)/shard_map/dot_general | solution.py:105
  323.5 5.1 %all-to-all-start.12 = ((bf16[4,36,2048]{2,1,0:T(8,128)(2,1)}), bf16[4,36,2048]{2,1,0:T(8,128)(2,1)S(1)}, u32[]{:S(2)}, u32[]{:S(2)}) async-start(bf16[4,36,2048]{2,1,0:T(8,128)(2,1)} %reshape.197), calls=%async_computation.12 | async-start | bytes 1310720 | tf_op jit(solution)/shard_map/all_to_all | solution.py:47
  328.6 21.4 %multiply_reduce_fusion.2 = (f32[]{:T(128)}, f32[]{:T(128)}, f32[]{:T(128)}, f32[]{:T(128)}, f32[3584,2048]{1,0:T(8,128)}) fusion(f32[3584,2048]{1,0:T(8,128)} %fusion.91, bf16[144,3584]{1,0:T(8,128)(2,1)} %fusion.37, bf16[144,2048]{1,0:T(8,128)(2,1)S(1)} %copy-done.2), kind=kOutput, calls=%fused_computation.16 | convolution fusion | flops 2172649472 | bytes 60342288 | tf_op jit(solution)/shard_map/rf,rd->fd/dot_general | solution.py:104
  355.7 39.8 %psum.16 = f32[]{:T(128)} all-reduce(f32[]{:T(128)S(6)} %add.143), channel_id=1, replica_groups=mesh['section'=4,'expert'=2,'dp'=4] {'section','expert','dp'}, use_global_device_ids=true, to_apply=%region_24.28 | all-reduce | flops 1 | bytes 8 | tf_op jit(solution)/shard_map/psum | solution.py:170
  397.8 5.7 %reshape.348 = bf16[2,2,73728]{2,1,0:T(2,128)(2,1)} reshape(bf16[2048,1,4,36]{3,2,1,0:T(4,128)(2,1)S(1)} %bitcast.144) | data formatting | bytes 1179648
  403.5 3.5 all-to-all-start.5
  407.0 47.9 %fusion = (bf16[1,1,3584,2048]{3,2,1,0:T(8,128)(2,1)}, bf16[1,1,3584,2048]{3,2,1,0:T(8,128)(2,1)}) fusion(f32[3584,2048]{1,0:T(8,128)} %fusion.91, f32[3584,2048]{1,0:T(8,128)} %get-tuple-element.41, f32[]{:T(128)S(6)} %div.72, f32[3584,2048]{1,0:T(8,128)} %fusion.60, f32[3584,2048]{1,0:T(8,128)} %get-tuple-element.42), kind=kLoop, calls=%fused_computation.22 | loop fusion | flops 44040192 | bytes 146800640 | tf_op jit(solution)/shard_map/broadcast_in_dim | solution.py:182
  456.4 5.7 %reshape.352 = bf16[2,2,73728]{2,1,0:T(2,128)(2,1)} reshape(bf16[2048,1,4,36]{3,2,1,0:T(4,128)(2,1)S(1)} %bitcast.145) | data formatting | bytes 1179648
  462.1 3.7 all-to-all-start.13
  465.8 6.0 %reshape.349 = bf16[2048,1,4,36]{3,2,1,0:T(4,128)(2,1)S(1)} reshape(bf16[2,2,73728]{2,1,0:T(2,128)(2,1)S(1)} %all-to-all-done.5) | data formatting | bytes 1179648
  479.2 6.0 %reshape.353 = bf16[2048,1,4,36]{3,2,1,0:T(4,128)(2,1)S(1)} reshape(bf16[2,2,73728]{2,1,0:T(2,128)(2,1)S(1)} %all-to-all-done.13) | data formatting | bytes 1179648
  (212 shorter events, 66.6 us)
Async XLA Ops:
  9.6 6.5 %copy-start.28 = (s32[1,2,64,2]{2,3,1,0:T(2,128)S(1)}, s32[1,2,64,2]{2,3,1,0:T(2,128)}, u32[]{:S(2)}) copy-start(s32[1,2,64,2]{2,3,1,0:T(2,128)} %param.22) | copy-start | bytes 3076
  9.7 9.0 %copy-start.29 = (f32[1,2,64,2]{2,3,1,0:T(2,128)S(1)}, f32[1,2,64,2]{2,3,1,0:T(2,128)}, u32[]{:S(2)}) copy-start(f32[1,2,64,2]{2,3,1,0:T(2,128)} %param.20) | copy-start | bytes 3076
  9.7 9.0 %copy-start.30 = (f32[1,2,64,2]{2,3,1,0:T(2,128)S(1)}, f32[1,2,64,2]{2,3,1,0:T(2,128)}, u32[]{:S(2)}) copy-start(f32[1,2,64,2]{2,3,1,0:T(2,128)} %param.23) | copy-start | bytes 3076
  9.8 14.0 %copy-start.10 = (bf16[1,64,1024]{2,1,0:T(8,128)(2,1)S(1)}, bf16[1,64,1024]{2,1,0:T(8,128)(2,1)}, u32[]{:S(2)}) copy-start(bf16[1,64,1024]{2,1,0:T(8,128)(2,1)} %param.24) | copy-start | bytes 393220
  10.8 35.2 %all-to-all-start = ((bf16[4,36,2048]{2,1,0:T(8,128)(2,1)}), bf16[4,36,2048]{2,1,0:T(8,128)(2,1)S(1)}, u32[]{:S(2)}, u32[]{:S(2)}) async-start(bf16[4,36,2048]{2,1,0:T(8,128)(2,1)} %reshape.173), calls=%async_computation | async-start | bytes 1310720 | tf_op jit(solution)/shard_map/all_to_all | solution.py:73
  17.2 22.7 %copy-start.21 = (pred[144]{0:T(512)(128)(4,1)}, pred[144]{0:T(512)(128)(4,1)S(1)}, u32[]{:S(2)}) copy-start(pred[144]{0:T(512)(128)(4,1)S(1)} %fusion.76) | copy-start | bytes 436
  30.4 1.5 copy-start.15
  46.0 15.4 %all-to-all-start.7 = ((bf16[4,36,2048]{2,1,0:T(8,128)(2,1)}), bf16[4,36,2048]{2,1,0:T(8,128)(2,1)S(1)}, u32[]{:S(2)}, u32[]{:S(2)}) async-start(bf16[4,36,2048]{2,1,0:T(8,128)(2,1)} %reshape.187), calls=%async_computation.7 | async-start | bytes 1310720 | tf_op jit(solution)/shard_map/all_to_all | solution.py:93
  61.5 32.2 %all-to-all-start.6 = ((bf16[4,36,2048]{2,1,0:T(8,128)(2,1)}), bf16[4,36,2048]{2,1,0:T(8,128)(2,1)S(1)}, u32[]{:S(2)}, u32[]{:S(2)}) async-start(bf16[4,36,2048]{2,1,0:T(8,128)(2,1)} %reshape.185), calls=%async_computation.6 | async-start | bytes 1310720 | tf_op jit(solution)/shard_map/all_to_all | solution.py:94
  83.3 10.4 %copy-start = (bf16[144,2048]{1,0:T(8,128)(2,1)}, bf16[144,2048]{1,0:T(8,128)(2,1)S(1)}, u32[]{:S(2)}) copy-start(bf16[144,2048]{1,0:T(8,128)(2,1)S(1)} %reshape.188) | copy-start | bytes 1769476
  93.7 27.2 %all-to-all-start.11 = ((bf16[4,36,2048]{2,1,0:T(8,128)(2,1)}), bf16[4,36,2048]{2,1,0:T(8,128)(2,1)}, u32[]{:S(2)}, u32[]{:S(2)}) async-start(bf16[4,36,2048]{2,1,0:T(8,128)(2,1)} %reshape.195), calls=%async_computation.11 | async-start | bytes 1310720 | tf_op jit(solution)/shard_map/all_to_all | solution.py:93
  120.9 19.9 %all-to-all-start.1 = ((bf16[4,36,2048]{2,1,0:T(8,128)(2,1)}), bf16[4,36,2048]{2,1,0:T(8,128)(2,1)}, u32[]{:S(2)}, u32[]{:S(2)}) async-start(bf16[4,36,2048]{2,1,0:T(8,128)(2,1)} %reshape.175), calls=%async_computation.1 | async-start | bytes 1310720 | tf_op jit(solution)/shard_map/all_to_all | solution.py:47
  140.8 26.9 %all-to-all-start.8 = ((bf16[4,36,2048]{2,1,0:T(8,128)(2,1)}), bf16[4,36,2048]{2,1,0:T(8,128)(2,1)}, u32[]{:S(2)}, u32[]{:S(2)}) async-start(bf16[4,36,2048]{2,1,0:T(8,128)(2,1)} %reshape.189), calls=%async_computation.8 | async-start | bytes 1310720 | tf_op jit(solution)/shard_map/all_to_all | solution.py:47
  161.9 9.7 %copy-start.1 = (bf16[144,2048]{1,0:T(8,128)(2,1)S(1)}, bf16[144,2048]{1,0:T(8,128)(2,1)}, u32[]{:S(2)}) copy-start(bf16[144,2048]{1,0:T(8,128)(2,1)} %reshape.196) | copy-start | bytes 1769476
  167.7 24.1 %all-to-all-start.2 = ((bf16[2,2,73728]{2,1,0:T(2,128)(2,1)}), bf16[2,2,73728]{2,1,0:T(2,128)(2,1)S(1)}, u32[]{:S(2)}, u32[]{:S(2)}) async-start(bf16[2,2,73728]{2,1,0:T(2,128)(2,1)} %reshape.346), calls=%async_computation.2 | async-start | bytes 1179648 | tf_op jit(solution)/shard_map/all_to_all | solution.py:48
  191.8 0.8 copy-start.3
  192.6 19.6 %all-to-all-start.9 = ((bf16[2,2,73728]{2,1,0:T(2,128)(2,1)}), bf16[2,2,73728]{2,1,0:T(2,128)(2,1)S(1)}, u32[]{:S(2)}, u32[]{:S(2)}) async-start(bf16[2,2,73728]{2,1,0:T(2,128)(2,1)} %reshape.350), calls=%async_computation.9 | async-start | bytes 1179648 | tf_op jit(solution)/shard_map/all_to_all | solution.py:48
  207.3 0.8 copy-start.26
  208.1 0.8 copy-start.17
  208.1 1.5 copy-start.9
  210.2 15.4 %collective-permute-start = (bf16[64,1024]{1,0:T(8,128)(2,1)}, bf16[64,1024]{1,0:T(8,128)(2,1)}, u32[]{:S(2)}, u32[]{:S(2)}) collective-permute-start(bf16[64,1024]{1,0:T(8,128)(2,1)} %fusion.70), channel_id=1, source_target_pairs={{0,8},{8,16},{16,24},{1,9},{9,17},{17,25},{2,10},{10,18},{18,26},{... | collective-permute-start | bytes 393224 | tf_op jit(solution)/shard_map/ppermute | solution.py:20
  222.4 0.8 copy-start.27
  223.2 2.4 copy-start.18
  224.3 1.4 copy-start.4
  224.4 14.9 %collective-permute-start.1 = (bf16[64,1024]{1,0:T(8,128)(2,1)S(1)}, bf16[64,1024]{1,0:T(8,128)(2,1)S(1)}, u32[]{:S(2)}, u32[]{:S(2)}) collective-permute-start(bf16[64,1024]{1,0:T(8,128)(2,1)S(1)} %fusion.73), channel_id=1, source_target_pairs={{8,0},{16,8},{24,16},{9,1},{17,9},{25,17},{10,2},{18,10},{26,18},{... | collective-permute-start | bytes 393224 | tf_op jit(solution)/shard_map/ppermute | solution.py:20
  225.7 6.6 %copy-start.7 = (bf16[64,1024]{1,0:T(8,128)(2,1)}, bf16[64,1024]{1,0:T(8,128)(2,1)S(1)}, u32[]{:S(2)}) copy-start(bf16[64,1024]{1,0:T(8,128)(2,1)S(1)} %bitcast_select_fusion.1) | copy-start | bytes 393220
  231.4 1.0 copy-start.23
  231.4 1.0 copy-start.31
  232.4 6.9 %copy-start.19 = (bf16[1,64,1024]{2,1,0:T(8,128)(2,1)S(1)}, bf16[1,64,1024]{2,1,0:T(8,128)(2,1)}, u32[]{:S(2)}) copy-start(bf16[1,64,1024]{2,1,0:T(8,128)(2,1)} %param.25) | copy-start | bytes 393220
  233.5 19.8 %all-to-all-start.3 = ((bf16[4,36,2048]{2,1,0:T(8,128)(2,1)}), bf16[4,36,2048]{2,1,0:T(8,128)(2,1)S(1)}, u32[]{:S(2)}, u32[]{:S(2)}) async-start(bf16[4,36,2048]{2,1,0:T(8,128)(2,1)} %reshape.179), calls=%async_computation.3 | async-start | bytes 1310720 | tf_op jit(solution)/shard_map/all_to_all | solution.py:73
  245.9 1.0 copy-start.20
  245.9 1.0 copy-start.22
  253.3 21.7 %all-to-all-start.10 = ((bf16[4,36,2048]{2,1,0:T(8,128)(2,1)}), bf16[4,36,2048]{2,1,0:T(8,128)(2,1)S(1)}, u32[]{:S(2)}, u32[]{:S(2)}) async-start(bf16[4,36,2048]{2,1,0:T(8,128)(2,1)} %reshape.193), calls=%async_computation.10 | async-start | bytes 1310720 | tf_op jit(solution)/shard_map/all_to_all | solution.py:94
  275.1 48.4 %all-to-all-start.4 = ((bf16[4,36,2048]{2,1,0:T(8,128)(2,1)}), bf16[4,36,2048]{2,1,0:T(8,128)(2,1)S(1)}, u32[]{:S(2)}, u32[]{:S(2)}) async-start(bf16[4,36,2048]{2,1,0:T(8,128)(2,1)} %reshape.181), calls=%async_computation.4 | async-start | bytes 1310720 | tf_op jit(solution)/shard_map/all_to_all | solution.py:47
  282.3 12.0 %copy-start.6 = (f32[144,3584]{1,0:T(8,128)S(1)}, f32[144,3584]{1,0:T(8,128)}, u32[]{:S(2)}) copy-start(f32[144,3584]{1,0:T(8,128)} %fusion.12) | copy-start | bytes 6193156
  322.5 6.1 %copy-start.2 = (bf16[144,2048]{1,0:T(8,128)(2,1)S(1)}, bf16[144,2048]{1,0:T(8,128)(2,1)}, u32[]{:S(2)}) copy-start(bf16[144,2048]{1,0:T(8,128)(2,1)} %reshape.196) | copy-start | bytes 1769476
  323.5 80.0 %all-to-all-start.12 = ((bf16[4,36,2048]{2,1,0:T(8,128)(2,1)}), bf16[4,36,2048]{2,1,0:T(8,128)(2,1)S(1)}, u32[]{:S(2)}, u32[]{:S(2)}) async-start(bf16[4,36,2048]{2,1,0:T(8,128)(2,1)} %reshape.197), calls=%async_computation.12 | async-start | bytes 1310720 | tf_op jit(solution)/shard_map/all_to_all | solution.py:47
  328.6 26.4 %copy-start.5 = (f32[64,1024]{1,0:T(8,128)S(1)}, f32[64,1024]{1,0:T(8,128)}, u32[]{:S(2)}) copy-start(f32[64,1024]{1,0:T(8,128)} %copy-done.4) | copy-start | bytes 786436
  328.6 26.4 %copy-start.11 = (bf16[1,64,1024]{2,1,0:T(8,128)(2,1)S(1)}, bf16[1,64,1024]{2,1,0:T(8,128)(2,1)}, u32[]{:S(2)}) copy-start(bf16[1,64,1024]{2,1,0:T(8,128)(2,1)} %param.24) | copy-start | bytes 393220
  403.5 58.7 %all-to-all-start.5 = ((bf16[2,2,73728]{2,1,0:T(2,128)(2,1)}), bf16[2,2,73728]{2,1,0:T(2,128)(2,1)S(1)}, u32[]{:S(2)}, u32[]{:S(2)}) async-start(bf16[2,2,73728]{2,1,0:T(2,128)(2,1)} %reshape.348), calls=%async_computation.5 | async-start | bytes 1179648 | tf_op jit(solution)/shard_map/all_to_all | solution.py:48
  462.1 17.1 %all-to-all-start.13 = ((bf16[2,2,73728]{2,1,0:T(2,128)(2,1)}), bf16[2,2,73728]{2,1,0:T(2,128)(2,1)S(1)}, u32[]{:S(2)}, u32[]{:S(2)}) async-start(bf16[2,2,73728]{2,1,0:T(2,128)(2,1)} %reshape.352), calls=%async_computation.13 | async-start | bytes 1179648 | tf_op jit(solution)/shard_map/all_to_all | solution.py:48
  476.1 1.0 copy-start.25
  477.0 0.8 copy-start.16
  477.1 1.5 copy-start.8
  489.7 1.0 copy-start.24
  490.7 1.1 copy-start.12
  490.7 1.1 copy-start.14
  490.7 1.9 copy-start.13
where the time goes:
time: 501 us; the launch traced here: 494 us
  matrix products  155 us (31%)
  local copies, waits for them, and re-layouts  99.8 us (20%)
  starting transfers between devices  75.7 us (15%)
  blocking collectives  70.8 us (14%)
  other arithmetic  69.7 us (14%)
  waiting for transfers between devices  14.4 us (3%)
  between operations  7.84 us (2%)
    unnamed x72, local copies, waits for them, and re-layouts  49.1 us
    broadcast_in_dim x1, other arithmetic, on_device(): gate_grad = (gate_total * factor).astype(jnp.bfloat16)[None, None]  47.9 us
    psum x1, blocking collectives, on_device(): squares = squares + lax.psum(growth, ('section', 'expert', 'dp'))  39.8 us
    dot_general x2, matrix products, backward_layer(): jnp.einsum('rf,rd->fd', slope_grad, flat_in, preferred_element_type=jnp.f...  34 us
    dot_general x2, matrix products, backward_layer(): jnp.einsum('rf,rd->fd', hidden, flat_grad, preferred_element_type=jnp.flo...  33.2 us
    dot_general x2, matrix products, forward_layer(): jnp.dot(hidden, down_weight, preferred_element_type=jnp.float32)  26.9 us
    all_to_all x4, starting transfers between devices, collect(): lax.all_to_all(partial_out, 'dp', split_axis=0, concat_axis=0, tiled=True)  22.8 us
    dot_general x2, matrix products, backward_layer(): jnp.einsum('rd,fd->rf', flat_grad, down_weight, preferred_element_type=jn...  22.6 us
  transfers between devices with their start and end apart: 16, of which 3 were waited for; matrix products, arithmetic and copies ran while one was open for 62% of the time, Pallas kernels for 0%

commit v1 on v0

v1 whole, which is shorter than its diff:
```python
import functools
import math

import jax
import jax.numpy as jnp
from jax import lax
from jax.experimental import pallas as pl
from jax.experimental.pallas import tpu as pltpu
from jax.sharding import PartitionSpec as P

CAP = 36
SLOTS = -(-CAP // 8) * 8

f32 = jnp.float32
bf16 = jnp.bfloat16
VMEM_LIMIT = 56 * 1024 * 1024


def nt(a, b):
    return lax.dot_general(a, b, (((1,), (1,)), ((), ())), preferred_element_type=f32)


def nn(a, b):
    return lax.dot_general(a, b, (((1,), (0,)), ((), ())), preferred_element_type=f32)


def tn(a, b):
    return lax.dot_general(a, b, (((0,), (0,)), ((), ())), preferred_element_type=f32)


def shifted(value, axis, steps):
    count = lax.axis_size(axis)
    initial, last = (max(0, -steps), min(count, count - steps))
    return lax.ppermute(value, axis, [(source, source + steps) for source in range(initial, last)])


def slot_targets(experts):
    tokens = experts.shape[1]
    same = experts[:, :, :, None, None] == experts[:, None, None, :, :]
    earlier = jnp.arange(tokens)[:, None] > jnp.arange(tokens)[None, :]
    place = jnp.sum((same & earlier[None, :, None, :, None]).astype(jnp.int32), axis=(3, 4))
    return experts * SLOTS + place


def picks(rows, target):
    slot = lax.broadcasted_iota(jnp.int32, (rows, target.shape[-1]), 0)
    return slot == target[0:1], slot == target[1:2]


def fill(out_ref, one_hot, pieces_ref, first, tokens, gate=None):
    width = pieces_ref.shape[-1]
    for piece in range(pieces_ref.shape[0]):
        rows = nn(one_hot, pieces_ref[piece, first : first + tokens, :])
        if gate is not None:
            rows = rows * gate
        out_ref[:, piece * width : (piece + 1) * width] = rows.astype(bf16)


def step_dispatch_kernel(tokens, target_f, target_b, gates_b, pieces, x_ref, s_ref):
    first, second = picks(x_ref.shape[0], target_f[...])
    fill(x_ref, (first | second).astype(f32).astype(bf16), pieces, 0, tokens)
    first, second = picks(s_ref.shape[0], target_b[...])
    gate = jnp.sum(
        jnp.where(first, gates_b[0:1, :], 0.0) + jnp.where(second, gates_b[1:2, :], 0.0),
        axis=1,
        keepdims=True,
    )
    fill(s_ref, (first | second).astype(f32).astype(bf16), pieces, tokens, tokens, gate)


def saved_dispatch_kernel(tokens, target, pieces, *outs):
    for tick, out_ref in enumerate(outs):
        first, second = picks(out_ref.shape[0], target[tick])
        fill(out_ref, (first | second).astype(f32).astype(bf16), pieces, tick * tokens, tokens)


def combine_kernel(target_f, gates_f, target_b, r_f, r_b, base_f, base_b, out_f, out_b):
    tokens, slots = base_f.shape[0], r_f.shape[0]
    slot = lax.broadcasted_iota(jnp.int32, (tokens, slots), 1)
    total = base_f[...].astype(f32)
    for k in range(2):
        pick = (slot == target_f[:, k : k + 1]).astype(f32).astype(bf16)
        total += gates_f[:, k : k + 1] * nn(pick, r_f[...])
    out_f[...] = total.astype(bf16)
    pick = ((slot == target_b[:, 0:1]) | (slot == target_b[:, 1:2])).astype(f32).astype(bf16)
    out_b[...] = (base_b[...].astype(f32) + nn(pick, r_b[...])).astype(bf16)


def put_pieces(out_ref, acc_ref):
    width = out_ref.shape[-1]
    for piece in range(out_ref.shape[0]):
        out_ref[piece] = acc_ref[:, piece * width : (piece + 1) * width].astype(bf16)


def first_step_kernel(
    xf, xb0, xb1, s0, gate, down, out_f, out_b, hid, slope, tilt, xs, acc_f, acc_b
):
    rows = xf.shape[0]
    step = pl.program_id(0)

    @pl.when(step == 0)
    def _():
        xs[0:rows, :] = xf[...]
        xs[rows : 2 * rows, :] = xb0[...]
        xs[2 * rows : 3 * rows, :] = xb1[...]
        acc_f[...] = jnp.zeros_like(acc_f)
        acc_b[...] = jnp.zeros_like(acc_b)

    pre = nt(xs[...], gate[...])
    sig = 1.0 / (1.0 + jnp.exp(-pre))
    hidden = (pre * sig).astype(bf16)
    hid[...] = hidden[rows:]
    acc_f[...] += nn(hidden[:rows], down[...])
    bend = sig[rows:] * (1.0 + pre[rows:] * (1.0 - sig[rows:]))
    tilt[...] = bend[rows:]
    through = nt(s0[...], down[...])
    sl = (through * bend[:rows]).astype(bf16)
    slope[...] = sl
    acc_b[...] += nn(sl, gate[...])

    @pl.when(step == pl.num_programs(0) - 1)
    def _():
        put_pieces(out_f, acc_f)
        put_pieces(out_b, acc_b)


def second_step_kernel(
    xf, s1, s0, xb0, xb1, gate, down, hid, slope0, tilt, out_f, out_b, slope1, squares,
    acc_f, acc_b, gram_h, gram_l,
):
    rows = xf.shape[0]
    step = pl.program_id(0)

    @pl.when(step == 0)
    def _():
        acc_f[...] = jnp.zeros_like(acc_f)
        acc_b[...] = jnp.zeros_like(acc_b)
        gram_h[...] = jnp.zeros_like(gram_h)
        gram_l[...] = jnp.zeros_like(gram_l)

    pre = nt(xf[...], gate[...])
    hidden = (pre / (1.0 + jnp.exp(-pre))).astype(bf16)
    acc_f[...] += nn(hidden, down[...])
    through = nt(s1[...], down[...])
    sl = (through * tilt[...]).astype(bf16)
    slope1[...] = sl
    acc_b[...] += nn(sl, gate[...])
    both = hid[...]
    gram_h[...] += nt(both, both)
    slopes = jnp.concatenate([slope0[...], sl], axis=0)
    gram_l[...] += nt(slopes, slopes)

    @pl.when(step == pl.num_programs(0) - 1)
    def _():
        put_pieces(out_f, acc_f)
        put_pieces(out_b, acc_b)
        scaled = jnp.concatenate([s0[...], s1[...]], axis=0)
        stored = jnp.concatenate([xb0[...], xb1[...]], axis=0)
        total = jnp.sum(gram_h[...] * nt(scaled, scaled) + gram_l[...] * nt(stored, stored))
        squares[...] = jnp.full(squares.shape, total, f32)


def grad_kernel(factor, xb0, xb1, s0, s1, hid, slope0, slope1, gate_out, down_out):
    rows = xb0.shape[0]
    scale = factor[0]
    down_sum = tn(hid[0:rows, :], s0[...]) + tn(hid[rows : 2 * rows, :], s1[...])
    down_out[...] = (down_sum * scale).astype(bf16)
    gate_sum = tn(slope0[...], xb0[...]) + tn(slope1[...], xb1[...])
    gate_out[...] = (gate_sum * scale).astype(bf16)


def params():
    return pltpu.CompilerParams(
        dimension_semantics=("arbitrary",), vmem_limit_bytes=VMEM_LIMIT
    )


def plain(kernel, shapes, name):
    return pl.pallas_call(
        kernel,
        out_shape=[jax.ShapeDtypeStruct(s, bf16) for s in shapes],
        name=name,
        compiler_params=pltpu.CompilerParams(vmem_limit_bytes=VMEM_LIMIT),
    )


def whole_spec(array):
    return pl.BlockSpec(array.shape, lambda i: (0,) * len(array.shape))


def on_device(
    fwd_input,
    fresh_input,
    fwd_experts,
    fwd_gates,
    bwd_saved,
    bwd_experts,
    bwd_gates,
    out_grad,
    fresh_grad,
    gate_proj,
    down_proj,
):
    gate_weight = gate_proj[0, 0]
    down_weight = down_proj[0, 0]
    hidden_units, width = gate_weight.shape
    section_count = lax.axis_size("section")
    expert_count = lax.axis_size("dp")
    feature_parts = lax.axis_size("expert")
    section_index = lax.axis_index("section")
    is_first = section_index == 0
    is_last = section_index == section_count - 1
    tick_count, tokens = fwd_experts.shape[1], fwd_experts.shape[2]
    part = fwd_input.shape[-1]
    rows = expert_count * SLOTS
    block = 512 if hidden_units % 512 == 0 else hidden_units
    steps = hidden_units // block

    targets_f = slot_targets(fwd_experts[0])
    targets_b = slot_targets(bwd_experts[0])
    lanes_f = jnp.swapaxes(targets_f, 1, 2)
    lanes_b = jnp.swapaxes(targets_b, 1, 2)
    gate_lanes_b = jnp.swapaxes(bwd_gates[0], 1, 2)

    def over_dp(value):
        return lax.all_to_all(value, "dp", split_axis=0, concat_axis=0, tiled=True)

    def dispatch(tick, input_part, grad_part):
        pieces = lax.all_gather(jnp.concatenate([input_part, grad_part], axis=0), "expert", axis=0)
        x, s = plain(
            functools.partial(step_dispatch_kernel, tokens),
            [(rows, width)] * 2,
            "step_dispatch",
        )(lanes_f[tick], lanes_b[tick], gate_lanes_b[tick], pieces)
        return over_dp(x), over_dp(s)

    def collect(tick, partial_f, partial_b, input_part, grad_part):
        swapped = lax.all_to_all(
            jnp.concatenate([partial_f, partial_b], axis=1),
            "expert", split_axis=0, concat_axis=0, tiled=True,
        )
        summed = jnp.sum(swapped.astype(f32), axis=0).astype(bf16)
        r_f, r_b = over_dp(summed[:rows]), over_dp(summed[rows:])
        return plain(combine_kernel, [(tokens, part)] * 2, "combine")(
            targets_f[tick], fwd_gates[0, tick], targets_b[tick], r_f, r_b, input_part, grad_part
        )

    saved_pieces = lax.all_gather(bwd_saved[0].reshape(tick_count * tokens, part), "expert", axis=0)
    stored = plain(
        functools.partial(saved_dispatch_kernel, tokens),
        [(rows, width)] * tick_count,
        "saved_dispatch",
    )(lanes_b, saved_pieces)
    stored0, stored1 = [over_dp(value) for value in stored]

    input_part, grad_part = fwd_input[0], out_grad[0]
    x0, scaled0 = dispatch(0, input_part, grad_part)

    def unit_block(count):
        return pl.BlockSpec((count, block), lambda i: (0, i))

    weight_spec = pl.BlockSpec((block, width), lambda i: (i, 0))
    pieces_shape = jax.ShapeDtypeStruct((feature_parts, rows, part), bf16)
    pieces_spec = whole_spec(pieces_shape)
    row_spec = whole_spec(x0)
    matmul = 2 * rows * hidden_units * width
    weight_bytes = 4 * hidden_units * width
    out_f, out_b, hid, slope0, tilt = pl.pallas_call(
        first_step_kernel,
        grid=(steps,),
        in_specs=[row_spec] * 4 + [weight_spec] * 2,
        out_specs=[pieces_spec] * 2 + [unit_block(2 * rows), unit_block(rows), unit_block(rows)],
        out_shape=[
            pieces_shape,
            pieces_shape,
            jax.ShapeDtypeStruct((2 * rows, hidden_units), bf16),
            jax.ShapeDtypeStruct((rows, hidden_units), bf16),
            jax.ShapeDtypeStruct((rows, hidden_units), f32),
        ],
        scratch_shapes=[
            pltpu.VMEM((3 * rows, width), bf16),
            pltpu.VMEM((rows, width), f32),
            pltpu.VMEM((rows, width), f32),
        ],
        compiler_params=params(),
        cost_estimate=pl.CostEstimate(
            flops=6 * matmul, bytes_accessed=weight_bytes, transcendentals=0
        ),
        name="first_step",
    )(x0, stored0, stored1, scaled0, gate_weight, down_weight)
    produced0, returned0 = collect(0, out_f, out_b, input_part, grad_part)

    arriving = shifted(produced0, "section", 1)
    leaving = shifted(returned0, "section", -1)
    input_part = jnp.where(is_first, fresh_input[0], arriving)
    grad_part = jnp.where(is_last, fresh_grad[0], leaving)
    x1, scaled1 = dispatch(1, input_part, grad_part)
    out_f, out_b, slope1, squares = pl.pallas_call(
        second_step_kernel,
        grid=(steps,),
        in_specs=[row_spec] * 5
        + [weight_spec] * 2
        + [unit_block(2 * rows), unit_block(rows), unit_block(rows)],
        out_specs=[pieces_spec] * 2
        + [unit_block(rows), pl.BlockSpec((8, 128), lambda i: (0, 0))],
        out_shape=[
            pieces_shape,
            pieces_shape,
            jax.ShapeDtypeStruct((rows, hidden_units), bf16),
            jax.ShapeDtypeStruct((8, 128), f32),
        ],
        scratch_shapes=[
            pltpu.VMEM((rows, width), f32),
            pltpu.VMEM((rows, width), f32),
            pltpu.VMEM((2 * rows, 2 * rows), f32),
            pltpu.VMEM((2 * rows, 2 * rows), f32),
        ],
        compiler_params=params(),
        cost_estimate=pl.CostEstimate(
            flops=4 * matmul, bytes_accessed=weight_bytes, transcendentals=0
        ),
        name="second_step",
    )(x1, scaled1, scaled0, stored0, stored1, gate_weight, down_weight, hid, slope0, tilt)

    everyone = lax.all_gather(squares, ("section", "expert", "dp"), axis=0)
    total = jnp.sum(everyone[:, 0, 0])
    clip_limit = 0.25 * math.sqrt(
        2.0 * section_count * expert_count * feature_parts * hidden_units * width
    )
    factor = clip_limit / jnp.maximum(jnp.sqrt(total), clip_limit)
    produced1, returned1 = collect(1, out_f, out_b, input_part, grad_part)

    gate_grad, down_grad = pl.pallas_call(
        grad_kernel,
        grid=(steps,),
        in_specs=[pl.BlockSpec(memory_space=pltpu.SMEM)]
        + [row_spec] * 4
        + [unit_block(2 * rows), unit_block(rows), unit_block(rows)],
        out_specs=[weight_spec] * 2,
        out_shape=[jax.ShapeDtypeStruct((hidden_units, width), bf16)] * 2,
        compiler_params=params(),
        cost_estimate=pl.CostEstimate(
            flops=4 * matmul, bytes_accessed=weight_bytes, transcendentals=0
        ),
        name="weight_grads",
    )(factor.reshape(1), stored0, stored1, scaled0, scaled1, hid, slope0, slope1)

    fwd_output = jnp.stack([produced0, produced1])[None]
    input_grad = jnp.stack([returned0, returned1])[None]
    return (fwd_output, input_grad, gate_grad[None, None], down_grad[None, None])


def solution(mesh):
    in_specs = (
        P("section", "dp", "expert"),
        P(None, "dp", "expert"),
        P("section", None, "dp", None),
        P("section", None, "dp", None),
        P("section", None, "dp", "expert"),
        P("section", None, "dp", None),
        P("section", None, "dp", None),
        P("section", "dp", "expert"),
        P(None, "dp", "expert"),
        P("section", "dp", "expert", None),
        P("section", "dp", "expert", None),
    )
    out_specs = (
        P("section", None, "dp", "expert"),
        P("section", None, "dp", "expert"),
        P("section", "dp", "expert", None),
        P("section", "dp", "expert", None),
    )
    return jax.shard_map(
        on_device, mesh=mesh, in_specs=in_specs, out_specs=out_specs, check_vma=False
    )
```

time: 501 us -> 389 us (0.78); the launches traced: 494 us -> 388 us
  blocking collectives: 70.8 us -> 244 us
  matrix products: 155 us -> 0 us
  local copies, waits for them, and re-layouts: 99.8 us -> 9.36 us
  Pallas kernels: 0 us -> 84.3 us
  other arithmetic: 69.7 us -> 10.8 us
  starting transfers between devices: 75.7 us -> 25.6 us
  between operations: 7.84 us -> 1.56 us
    all_to_all x0 -> x8, blocking collectives: none -> 156 us  [the longest x6 120 us: over_dp(): return lax.all_to_all(value, 'dp', split_axis=0, concat_axis=0, tiled=True)]
    dot_general x16 -> x0, matrix products: 155 us -> none  [the longest x2 34 us: backward_layer(): jnp.einsum('rf,rd->fd', slope_grad, flat_in, preferred_element_type=jnp.f...]
    pallas_call x0 -> x8, Pallas kernels: none -> 84.3 us  [the longest x1 27.4 us: on_device(): pl.pallas_call(second_step_kernel, grid=(steps,), in_specs=[row_spec] * 5...]
    all_gather x5 -> x4, blocking collectives: 31 us -> 88.9 us  [the longest x1 65.5 us: on_device(): everyone = lax.all_gather(squares, ('section', 'expert', 'dp'), axis=0)]
    all_to_all x14 -> x4, starting transfers between devices: 72.5 us -> 23 us  [over_dp(): return lax.all_to_all(value, 'dp', split_axis=0, concat_axis=0, tiled=True)]
    unnamed x72 -> x30, local copies, waits for them, and re-layouts: 49.1 us -> 1.51 us
    broadcast_in_dim x3 -> x2, other arithmetic: 49.4 us -> 3.26 us  [the longest x1 1.63 us: on_device(): fwd_output = jnp.stack([produced0, produced1])[None]]
    psum x1 -> x0, blocking collectives: 39.8 us -> none  [on_device(): squares = squares + lax.psum(growth, ('section', 'expert', 'dp'))]
  transfers between devices with their start and end apart: 16 -> 6, of which waited for: 3 -> 3; matrix products, arithmetic and copies ran while one was open for 62% -> 1% of each run, Pallas kernels for 0% -> 6%
where the time goes in v1:
time: 389 us; the launch traced here: 388 us
  blocking collectives  244 us (63%)
  Pallas kernels  84.3 us (22%)
  starting transfers between devices  25.6 us (7%)
  waiting for transfers between devices  11.9 us (3%)
  other arithmetic  10.8 us (3%)
  local copies, waits for them, and re-layouts  9.36 us (2%)
    all_to_all x6, blocking collectives, over_dp(): return lax.all_to_all(value, 'dp', split_axis=0, concat_axis=0, tiled=True)  120 us
    all_gather x1, blocking collectives, on_device(): everyone = lax.all_gather(squares, ('section', 'expert', 'dp'), axis=0)  65.5 us
    all_to_all x2, blocking collectives, collect(): lax.all_to_all(jnp.concatenate([partial_f, partial_b], axis=1), 'expert',...  35.4 us
    pallas_call x1, Pallas kernels, on_device(): pl.pallas_call(second_step_kernel, grid=(steps,), in_specs=[row_spec] * 5...  27.4 us
    pallas_call x1, Pallas kernels, on_device(): pl.pallas_call(first_step_kernel, grid=(steps,), in_specs=[row_spec] * 4...  24.7 us
    all_to_all x4, starting transfers between devices, over_dp(): return lax.all_to_all(value, 'dp', split_axis=0, concat_axis=0, tiled=True)  23 us
    pallas_call x1, Pallas kernels, on_device(): pl.pallas_call(grad_kernel, grid=(steps,), in_specs=[pl.BlockSpec(memory_...  20.4 us
    all_gather x2, blocking collectives, dispatch(): lax.all_gather(jnp.concatenate([input_part, grad_part], axis=0), 'expert'...  16.2 us
  transfers between devices with their start and end apart: 6, of which 3 were waited for; matrix products, arithmetic and copies ran while one was open for 1% of the time, Pallas kernels for 6%

profile of v1, /device:TPU:12, one launch (start us, length us, event | category | flops | bytes accessed | tf_op | source)
XLA Modules:
  0.0 387.9 jit_solution(13344165560547405917)
XLA Ops:
  0.7 1.3 slice_bitcast_fusion.5
  2.0 1.1 convert_reduce_fusion
  3.1 0.7 multiply_add_fusion
  3.8 0.7 multiply_add_fusion.1
  4.5 1.0 pad_maximum_fusion.2
  5.4 8.8 %all-gather = bf16[256,1024]{1,0:T(8,128)(2,1)} all-gather(bf16[128,1024]{1,0:T(8,128)(2,1)S(1)} %pad_maximum_fusion.2), channel_id=2, replica_groups=mesh['section'=4,'expert'=2,'dp'=4] {'expert'}, dimensions={0}, use_global_device_ids=true | all-gather | bytes 786432 | tf_op jit(solution)/shard_map/all_gather | solution.py:229
  14.9 2.4 step_dispatch.2
  17.3 20.1 %all_to_all.120 = bf16[4,40,2048]{2,1,0:T(8,128)(2,1)} all-to-all(bf16[4,40,2048]{2,1,0:T(8,128)(2,1)} %bitcast.104), channel_id=1, replica_groups=mesh['section'=4,'expert'=2,'dp'=4] {'dp'}, dimensions={0} | all-to-all | bytes 1310720 | tf_op jit(solution)/shard_map/all_to_all | solution.py:226
  37.3 5.3 %all-to-all-start = ((bf16[4,40,2048]{2,1,0:T(8,128)(2,1)}), bf16[4,40,2048]{2,1,0:T(8,128)(2,1)S(1)}, u32[]{:S(2)}, u32[]{:S(2)}) async-start(bf16[4,40,2048]{2,1,0:T(8,128)(2,1)} %bitcast.100), calls=%async_computation | async-start | bytes 1310720 | tf_op jit(solution)/shard_map/all_to_all | solution.py:226
  42.6 7.3 %all_gather.23.pieces = bf16[2,128,1024]{2,1,0:T(8,128)(2,1)} all-gather(bf16[1,128,1024]{2,1,0:T(8,128)(2,1)S(1)} %bitcast.110), channel_id=1, replica_groups=mesh['section'=4,'expert'=2,'dp'=4] {'expert'}, dimensions={0}, use_global_device_ids=true | all-gather | bytes 786432 | tf_op jit(solution)/shard_map/all_gather | solution.py:248
  49.9 2.4 saved_dispatch.1
  52.3 3.3 all-to-all-done
  55.7 22.6 %all_to_all.121 = bf16[4,40,2048]{2,1,0:T(8,128)(2,1)} all-to-all(bf16[4,40,2048]{2,1,0:T(8,128)(2,1)} %bitcast.102), channel_id=1, replica_groups=mesh['section'=4,'expert'=2,'dp'=4] {'dp'}, dimensions={0} | all-to-all | bytes 1310720 | tf_op jit(solution)/shard_map/all_to_all | solution.py:226
  78.2 20.5 %all_to_all.122 = bf16[4,40,2048]{2,1,0:T(8,128)(2,1)} all-to-all(bf16[4,40,2048]{2,1,0:T(8,128)(2,1)} %bitcast.101), channel_id=1, replica_groups=mesh['section'=4,'expert'=2,'dp'=4] {'dp'}, dimensions={0} | all-to-all | bytes 1310720 | tf_op jit(solution)/shard_map/all_to_all | solution.py:226
  98.7 24.7 %first_step.1 = (bf16[2,160,1024]{2,1,0:T(8,128)(2,1)}, bf16[2,160,1024]{2,1,0:T(8,128)(2,1)}, bf16[320,3584]{1,0:T(8,128)(2,1)}, bf16[160,3584]{1,0:T(8,128)(2,1)}, f32[160,3584]{1,0:T(8,128)}) custom-call(bf16[160,2048]{1,0:T(8,128)(2,1)} %bitcast.99, bf16[160,2048]{1,0:T(8,128)(2,1)} %bitcast.86, bf16[160,2048]{1,0:T(8,128)(2,1)} %bitcast.83, ...), custom_call_target="tpu_custom_call" | custom-call | flops 14092861440 | bytes 29360128 | tf_op jit(solution)/shard_map/first_step/pallas_call | solution.py:268
  123.5 1.4 pad_maximum_fusion
  124.9 16.4 %all_to_all.123 = bf16[2,320,1024]{2,1,0:T(8,128)(2,1)S(1)} all-to-all(bf16[2,320,1024]{2,1,0:T(8,128)(2,1)S(1)} %pad_maximum_fusion), channel_id=1, replica_groups=mesh['section'=4,'expert'=2,'dp'=4] {'expert'}, dimensions={0} | all-to-all | bytes 2621440 | tf_op jit(solution)/shard_map/all_to_all | solution.py:238
  141.6 0.8 fusion.1
  142.4 12.5 %all_to_all.124 = bf16[4,40,1024]{2,1,0:T(8,128)(2,1)} all-to-all(bf16[4,40,1024]{2,1,0:T(8,128)(2,1)S(1)} %bitcast.94), channel_id=1, replica_groups=mesh['section'=4,'expert'=2,'dp'=4] {'dp'}, dimensions={0} | all-to-all | bytes 655360 | tf_op jit(solution)/shard_map/all_to_all | solution.py:226
  154.9 5.1 %all-to-all-start.6 = ((bf16[4,40,1024]{2,1,0:T(8,128)(2,1)}), bf16[4,40,1024]{2,1,0:T(8,128)(2,1)S(1)}, u32[]{:S(2)}, u32[]{:S(2)}) async-start(bf16[4,40,1024]{2,1,0:T(8,128)(2,1)} %bitcast.28), calls=%async_computation.6 | async-start | bytes 655360 | tf_op jit(solution)/shard_map/all_to_all | solution.py:226
  159.9 0.7 copy.37.target_b
  160.6 0.7 copy.35.target_f
  161.4 0.7 copy.36.gates_f
  162.1 4.7 %all-to-all-done.6 = bf16[4,40,1024]{2,1,0:T(8,128)(2,1)S(1)} async-done(((bf16[4,40,1024]{2,1,0:T(8,128)(2,1)}), bf16[4,40,1024]{2,1,0:T(8,128)(2,1)S(1)}, u32[]{:S(2)}, u32[]{:S(2)}) %all-to-all-start.6) | async-done | bytes 327712 | tf_op jit(solution)/shard_map/all_to_all | solution.py:226
  166.8 0.7 copy-done.1
  167.5 2.2 combine.2
  169.7 1.3 collective-permute-start
  171.0 1.3 collective-permute-start.1
  172.4 3.8 collective-permute-done.1
  176.3 7.4 %all-gather.1 = bf16[256,1024]{1,0:T(8,128)(2,1)} all-gather(bf16[128,1024]{1,0:T(8,128)(2,1)S(1)} %pad_maximum_fusion.3), channel_id=3, replica_groups=mesh['section'=4,'expert'=2,'dp'=4] {'expert'}, dimensions={0}, use_global_device_ids=true | all-gather | bytes 786432 | tf_op jit(solution)/shard_map/all_gather | solution.py:229
  183.6 2.4 step_dispatch.3
  186.1 21.5 %all_to_all.125 = bf16[4,40,2048]{2,1,0:T(8,128)(2,1)} all-to-all(bf16[4,40,2048]{2,1,0:T(8,128)(2,1)} %bitcast.105), channel_id=1, replica_groups=mesh['section'=4,'expert'=2,'dp'=4] {'dp'}, dimensions={0} | all-to-all | bytes 1310720 | tf_op jit(solution)/shard_map/all_to_all | solution.py:226
  207.6 23.0 %all_to_all.126 = bf16[4,40,2048]{2,1,0:T(8,128)(2,1)} all-to-all(bf16[4,40,2048]{2,1,0:T(8,128)(2,1)} %bitcast.103), channel_id=1, replica_groups=mesh['section'=4,'expert'=2,'dp'=4] {'dp'}, dimensions={0} | all-to-all | bytes 1310720 | tf_op jit(solution)/shard_map/all_to_all | solution.py:226
  230.6 27.4 %second_step.1 = (bf16[2,160,1024]{2,1,0:T(8,128)(2,1)}, bf16[2,160,1024]{2,1,0:T(8,128)(2,1)}, bf16[160,3584]{1,0:T(8,128)(2,1)}, f32[8,128]{1,0:T(8,128)}) custom-call(bf16[160,2048]{1,0:T(8,128)(2,1)} %bitcast.91, bf16[160,2048]{1,0:T(8,128)(2,1)} %bitcast.89, bf16[160,2048]{1,0:T(8,128)(2,1)} %bitcast.81, bf16[160,2048]{1,0:T(8,128)(2,1)} %bitcast.87, ...), custom_call_target="tpu_custom_call" | custom-call | flops 9395240960 | bytes 29360128 | tf_op jit(solution)/shard_map/second_step/pallas_call | solution.py:298
  258.0 1.4 pad_maximum_fusion.1
  259.4 18.9 %all_to_all.127 = bf16[2,320,1024]{2,1,0:T(8,128)(2,1)S(1)} all-to-all(bf16[2,320,1024]{2,1,0:T(8,128)(2,1)S(1)} %pad_maximum_fusion.1), channel_id=1, replica_groups=mesh['section'=4,'expert'=2,'dp'=4] {'expert'}, dimensions={0} | all-to-all | bytes 2621440 | tf_op jit(solution)/shard_map/all_to_all | solution.py:238
  278.7 0.9 fusion
  279.6 5.6 %all-to-all-start.10 = ((bf16[4,40,1024]{2,1,0:T(8,128)(2,1)}), bf16[4,40,1024]{2,1,0:T(8,128)(2,1)S(1)}, u32[]{:S(2)}, u32[]{:S(2)}) async-start(bf16[4,40,1024]{2,1,0:T(8,128)(2,1)} %bitcast.45), calls=%async_computation.10 | async-start | bytes 655360 | tf_op jit(solution)/shard_map/all_to_all | solution.py:226
  285.1 0.7 copy.40.target_b
  285.9 0.7 copy.38.target_f
  286.6 0.7 copy.39.gates_f
  287.3 65.5 %all-gather.2 = f32[256,128]{1,0:T(8,128)S(1)} all-gather(f32[8,128]{1,0:T(8,128)S(1)} %copy-done.13), channel_id=4, replica_groups=mesh['section'=4,'expert'=2,'dp'=4] {'section','expert','dp'}, dimensions={0}, use_global_device_ids=true | all-gather | bytes 135168 | tf_op jit(solution)/shard_map/all_gather | solution.py:325
  354.1 7.1 %all-to-all-start.11 = ((bf16[4,40,1024]{2,1,0:T(8,128)(2,1)}), bf16[4,40,1024]{2,1,0:T(8,128)(2,1)S(1)}, u32[]{:S(2)}, u32[]{:S(2)}) async-start(bf16[4,40,1024]{2,1,0:T(8,128)(2,1)} %bitcast.47), calls=%async_computation.11 | async-start | bytes 655360 | tf_op jit(solution)/shard_map/all_to_all | solution.py:226
  361.2 20.4 %weight_grads.1 = (bf16[3584,2048]{1,0:T(8,128)(2,1)}, bf16[3584,2048]{1,0:T(8,128)(2,1)}) custom-call(f32[1]{0:T(128)} %bitcast.55.factor, bf16[160,2048]{1,0:T(8,128)(2,1)} %bitcast.88, bf16[160,2048]{1,0:T(8,128)(2,1)} %bitcast.85, bf16[160,2048]{1,0:T(8,128)(2,1)} %bitcast.82, bf16[160,2048]{1,0:T(8,128)(2,1)} %bitcast.90, ...), custom_call_target="tpu_custom_call" | custom-call | flops 9395240960 | bytes 29360128 | tf_op jit(solution)/shard_map/weight_grads/pallas_call | solution.py:333
  381.7 0.7 copy-done.2
  382.4 2.2 combine.3
  384.7 1.6 maximum_bitcast_fusion
  386.3 1.6 maximum_bitcast_fusion.1
  (42 shorter events, 2.0 us)
Async XLA Ops:
  0.6 42.0 %copy-start.6 = (bf16[1,2,64,1024]{3,2,1,0:T(8,128)(2,1)S(1)}, bf16[1,2,64,1024]{3,2,1,0:T(8,128)(2,1)}, u32[]{:S(2)}) copy-start(bf16[1,2,64,1024]{3,2,1,0:T(8,128)(2,1)} %param.15) | copy-start | bytes 786436
  3.8 46.1 %copy-start.11 = (s32[2,64,2]{1,2,0:T(2,128)}, s32[2,64,2]{1,2,0:T(2,128)S(1)}, u32[]{:S(2)}) copy-start(s32[2,64,2]{1,2,0:T(2,128)S(1)} %multiply_add_fusion) | copy-start | bytes 3076
  37.3 18.3 %all-to-all-start = ((bf16[4,40,2048]{2,1,0:T(8,128)(2,1)}), bf16[4,40,2048]{2,1,0:T(8,128)(2,1)S(1)}, u32[]{:S(2)}, u32[]{:S(2)}) async-start(bf16[4,40,2048]{2,1,0:T(8,128)(2,1)} %bitcast.100), calls=%async_computation | async-start | bytes 1310720 | tf_op jit(solution)/shard_map/all_to_all | solution.py:226
  55.6 43.1 %copy-start.5 = (bf16[4,40,2048]{2,1,0:T(8,128)(2,1)}, bf16[4,40,2048]{2,1,0:T(8,128)(2,1)S(1)}, u32[]{:S(2)}) copy-start(bf16[4,40,2048]{2,1,0:T(8,128)(2,1)S(1)} %all-to-all-done) | copy-start | bytes 1966084
  141.3 18.7 %copy-start.12 = (s32[2,64,2]{1,2,0:T(2,128)S(1)}, s32[2,64,2]{1,2,0:T(2,128)}, u32[]{:S(2)}) copy-start(s32[2,64,2]{1,2,0:T(2,128)} %copy-done.11) | copy-start | bytes 3076
  141.3 20.1 %copy-start.14 = (f32[1,2,64,2]{2,3,1,0:T(2,128)S(1)}, f32[1,2,64,2]{2,3,1,0:T(2,128)}, u32[]{:S(2)}) copy-start(f32[1,2,64,2]{2,3,1,0:T(2,128)} %param.14) | copy-start | bytes 3076
  141.6 30.7 %copy-start.7 = (bf16[1,64,1024]{2,1,0:T(8,128)(2,1)S(1)}, bf16[1,64,1024]{2,1,0:T(8,128)(2,1)}, u32[]{:S(2)}) copy-start(bf16[1,64,1024]{2,1,0:T(8,128)(2,1)} %param.12) | copy-start | bytes 393220
  141.6 34.6 %copy-start.8 = (bf16[1,64,1024]{2,1,0:T(8,128)(2,1)S(1)}, bf16[1,64,1024]{2,1,0:T(8,128)(2,1)}, u32[]{:S(2)}) copy-start(bf16[1,64,1024]{2,1,0:T(8,128)(2,1)} %param.19) | copy-start | bytes 393220
  154.9 11.9 %all-to-all-start.6 = ((bf16[4,40,1024]{2,1,0:T(8,128)(2,1)}), bf16[4,40,1024]{2,1,0:T(8,128)(2,1)S(1)}, u32[]{:S(2)}, u32[]{:S(2)}) async-start(bf16[4,40,1024]{2,1,0:T(8,128)(2,1)} %bitcast.28), calls=%async_computation.6 | async-start | bytes 655360 | tf_op jit(solution)/shard_map/all_to_all | solution.py:226
  166.8 0.7 copy-start.1
  169.7 2.6 collective-permute-start
  171.0 5.2 %collective-permute-start.1 = (bf16[64,1024]{1,0:T(8,128)(2,1)}, bf16[64,1024]{1,0:T(8,128)(2,1)S(1)}, u32[]{:S(2)}, u32[]{:S(2)}) collective-permute-start(bf16[64,1024]{1,0:T(8,128)(2,1)} %get-tuple-element.32), channel_id=1, source_target_pairs={{8,0},{16,8},{24,16},{9,1},{17,9},{25,17},{10,2},{18,10},{26,18},{... | collective-permute-start | bytes 393224 | tf_op jit(solution)/shard_map/ppermute | solution.py:34
  172.4 58.2 %copy-start.3 = (bf16[64,1024]{1,0:T(8,128)(2,1)}, bf16[64,1024]{1,0:T(8,128)(2,1)S(1)}, u32[]{:S(2)}) copy-start(bf16[64,1024]{1,0:T(8,128)(2,1)S(1)} %bitcast_select_fusion.1.base_f) | copy-start | bytes 393220
  176.2 81.8 %copy-start.4 = (bf16[64,1024]{1,0:T(8,128)(2,1)}, bf16[64,1024]{1,0:T(8,128)(2,1)S(1)}, u32[]{:S(2)}) copy-start(bf16[64,1024]{1,0:T(8,128)(2,1)S(1)} %bitcast_select_fusion.base_b) | copy-start | bytes 393220
  278.4 8.9 %copy-start.13 = (f32[8,128]{1,0:T(8,128)S(1)}, f32[8,128]{1,0:T(8,128)}, u32[]{:S(2)}) copy-start(f32[8,128]{1,0:T(8,128)} %get-tuple-element.42) | copy-start | bytes 12292
  279.6 74.5 %all-to-all-start.10 = ((bf16[4,40,1024]{2,1,0:T(8,128)(2,1)}), bf16[4,40,1024]{2,1,0:T(8,128)(2,1)S(1)}, u32[]{:S(2)}, u32[]{:S(2)}) async-start(bf16[4,40,1024]{2,1,0:T(8,128)(2,1)} %bitcast.45), calls=%async_computation.10 | async-start | bytes 655360 | tf_op jit(solution)/shard_map/all_to_all | solution.py:226
  354.1 27.6 %copy-start = (bf16[4,40,1024]{2,1,0:T(8,128)(2,1)}, bf16[4,40,1024]{2,1,0:T(8,128)(2,1)S(1)}, u32[]{:S(2)}) copy-start(bf16[4,40,1024]{2,1,0:T(8,128)(2,1)S(1)} %all-to-all-done.10) | copy-start | bytes 983044
  354.1 27.6 %all-to-all-start.11 = ((bf16[4,40,1024]{2,1,0:T(8,128)(2,1)}), bf16[4,40,1024]{2,1,0:T(8,128)(2,1)S(1)}, u32[]{:S(2)}, u32[]{:S(2)}) async-start(bf16[4,40,1024]{2,1,0:T(8,128)(2,1)} %bitcast.47), calls=%async_computation.11 | async-start | bytes 655360 | tf_op jit(solution)/shard_map/all_to_all | solution.py:226
  361.2 23.4 %copy-start.10 = (bf16[64,1024]{1,0:T(8,128)(2,1)S(1)}, bf16[64,1024]{1,0:T(8,128)(2,1)}, u32[]{:S(2)}) copy-start(bf16[64,1024]{1,0:T(8,128)(2,1)} %get-tuple-element.31) | copy-start | bytes 393220
  361.2 25.1 %copy-start.9 = (bf16[64,1024]{1,0:T(8,128)(2,1)S(1)}, bf16[64,1024]{1,0:T(8,128)(2,1)}, u32[]{:S(2)}) copy-start(bf16[64,1024]{1,0:T(8,128)(2,1)} %get-tuple-element.32) | copy-start | bytes 393220
  381.7 0.7 copy-start.2

commit v2 on v1

--- a/solution.py
+++ b/solution.py
@@ -28,12 +28,6 @@
     return lax.dot_general(a, b, (((0,), (0,)), ((), ())), preferred_element_type=f32)
 
 
-def shifted(value, axis, steps):
-    count = lax.axis_size(axis)
-    initial, last = (max(0, -steps), min(count, count - steps))
-    return lax.ppermute(value, axis, [(source, source + steps) for source in range(initial, last)])
-
-
 def slot_targets(experts):
     tokens = experts.shape[1]
     same = experts[:, :, :, None, None] == experts[:, None, None, :, :]
@@ -42,48 +36,282 @@
     return experts * SLOTS + place
 
 
-def picks(rows, target):
-    slot = lax.broadcasted_iota(jnp.int32, (rows, target.shape[-1]), 0)
-    return slot == target[0:1], slot == target[1:2]
-
-
-def fill(out_ref, one_hot, pieces_ref, first, tokens, gate=None):
-    width = pieces_ref.shape[-1]
-    for piece in range(pieces_ref.shape[0]):
-        rows = nn(one_hot, pieces_ref[piece, first : first + tokens, :])
-        if gate is not None:
-            rows = rows * gate
-        out_ref[:, piece * width : (piece + 1) * width] = rows.astype(bf16)
-
-
-def step_dispatch_kernel(tokens, target_f, target_b, gates_b, pieces, x_ref, s_ref):
-    first, second = picks(x_ref.shape[0], target_f[...])
-    fill(x_ref, (first | second).astype(f32).astype(bf16), pieces, 0, tokens)
-    first, second = picks(s_ref.shape[0], target_b[...])
-    gate = jnp.sum(
-        jnp.where(first, gates_b[0:1, :], 0.0) + jnp.where(second, gates_b[1:2, :], 0.0),
-        axis=1,
-        keepdims=True,
-    )
-    fill(s_ref, (first | second).astype(f32).astype(bf16), pieces, tokens, tokens, gate)
-
-
-def saved_dispatch_kernel(tokens, target, pieces, *outs):
-    for tick, out_ref in enumerate(outs):
-        first, second = picks(out_ref.shape[0], target[tick])
-        fill(out_ref, (first | second).astype(f32).astype(bf16), pieces, tick * tokens, tokens)
-
-
-def combine_kernel(target_f, gates_f, target_b, r_f, r_b, base_f, base_b, out_f, out_b):
-    tokens, slots = base_f.shape[0], r_f.shape[0]
-    slot = lax.broadcasted_iota(jnp.int32, (tokens, slots), 1)
-    total = base_f[...].astype(f32)
-    for k in range(2):
-        pick = (slot == target_f[:, k : k + 1]).astype(f32).astype(bf16)
-        total += gates_f[:, k : k + 1] * nn(pick, r_f[...])
-    out_f[...] = total.astype(bf16)
-    pick = ((slot == target_b[:, 0:1]) | (slot == target_b[:, 1:2])).astype(f32).astype(bf16)
-    out_b[...] = (base_b[...].astype(f32) + nn(pick, r_b[...])).astype(bf16)
+def ring(axis, step):
+    return lax.rem(lax.axis_index(axis) + step, lax.axis_size(axis))
+
+
+def greet(places):
+    barrier = pltpu.get_barrier_semaphore()
+    for place in places:
+        pl.semaphore_signal(
+            barrier, inc=1, device_id=place, device_id_type=pl.DeviceIdType.MESH
+        )
+    pl.semaphore_wait(barrier, len(places))
+
+
+def peers(axis):
+    return [{axis: ring(axis, step)} for step in range(1, lax.axis_size(axis))]
+
+
+def remote(source, target, send, recv, place):
+    copy = pltpu.make_async_remote_copy(
+        src_ref=source,
+        dst_ref=target,
+        send_sem=send,
+        recv_sem=recv,
+        device_id=place,
+        device_id_type=pl.DeviceIdType.MESH,
+    )
+    copy.start()
+    return copy
+
+
+def wait_all(copies):
+    for copy in copies:
+        copy.wait()
+
+
+def gather_pieces(source, pieces, send, recv):
+    me = lax.axis_index("expert")
+    copies = [
+        remote(source, pieces.at[me], send.at[step], recv.at[step], place)
+        for step, place in enumerate(peers("expert"))
+    ]
+    pieces[me] = source[...]
+    return copies
+
+
+def send_slots(out, buffer, pieces, target, gates, send, recv):
+    count, slots = out.shape[0], out.shape[1]
+    parts, tokens, part = pieces.shape
+    me = lax.axis_index("dp")
+    copies = []
+    for step in [*range(1, count), 0]:
+        home = ring("dp", step)
+        slot = lax.broadcasted_iota(jnp.int32, (slots, tokens), 0) + home * slots
+        first, second = slot == target[0:1], slot == target[1:2]
+        one_hot = (first | second).astype(f32).astype(bf16)
+        if gates is not None:
+            gate = jnp.sum(
+                jnp.where(first, gates[0:1], 0.0) + jnp.where(second, gates[1:2], 0.0),
+                axis=1,
+                keepdims=True,
+            )
+        for piece in range(parts):
+            rows = nn(one_hot, pieces[piece])
+            if gates is not None:
+                rows = rows * gate
+            columns = slice(piece * part, (piece + 1) * part)
+            if step:
+                buffer[step - 1, :, columns] = rows.astype(bf16)
+            else:
+                out[me, :, columns] = rows.astype(bf16)
+        if step:
+            copies.append(
+                remote(
+                    buffer.at[step - 1], out.at[me], send.at[step - 1], recv.at[step - 1],
+                    {"dp": home},
+                )
+            )
+    return copies
+
+
+def start_partials(partials, arrived, send, recv):
+    copies = {}
+    count = partials[0].shape[1]
+    for step in [*range(1, count), 0]:
+        home = ring("dp", step)
+        for stream, partial in enumerate(partials):
+            copies[stream, step] = [
+                remote(
+                    partial.at[place["expert"], home],
+                    arrived[stream].at[turn, step],
+                    send.at[stream, turn, step],
+                    recv.at[stream, turn, step],
+                    place,
+                )
+                for turn, place in enumerate(peers("expert"))
+            ]
+    return copies
+
+
+def finish_partials(copies, partials, arrived, buffers, returned, send, recv):
+    parts, count = partials[0].shape[0], partials[0].shape[1]
+    mine, me = lax.axis_index("expert"), lax.axis_index("dp")
+    leaving = []
+    for step in [*range(1, count), 0]:
+        home = ring("dp", step)
+        for stream, partial in enumerate(partials):
+            wait_all(copies[stream, step])
+            total = partial[mine, home].astype(f32)
+            for turn in range(parts - 1):
+                total += arrived[stream][turn, step].astype(f32)
+            if step:
+                buffers[stream][step - 1] = total.astype(bf16)
+                leaving.append(
+                    remote(
+                        buffers[stream].at[step - 1],
+                        returned[stream].at[me],
+                        send.at[stream, step - 1],
+                        recv.at[stream, step - 1],
+                        {"dp": home},
+                    )
+                )
+            else:
+                returned[stream][me] = total.astype(bf16)
+    return leaving
+
+
+def combined(base, returned, target, gates):
+    count, slots = returned.shape[0], returned.shape[1]
+    tokens = base.shape[0]
+    total = base.astype(f32)
+    for number in range(count):
+        slot = lax.broadcasted_iota(jnp.int32, (tokens, slots), 1) + number * slots
+        for k in range(2):
+            pick = (slot == target[:, k : k + 1]).astype(f32).astype(bf16)
+            rows = nn(pick, returned[number])
+            total += rows if gates is None else gates[:, k : k + 1] * rows
+    return total.astype(bf16)
+
+
+def enter_kernel(
+    lanes_f, lanes_b, gate_lanes_b, fwd, grad, saved, x0, s0, *rest
+):
+    ticks = saved.shape[0]
+    stored, (pieces, buffers, send_y, recv_y, send_z, recv_z) = rest[:ticks], rest[ticks:]
+    greet(peers("expert") + peers("dp"))
+    sources = [fwd, saved.at[0], grad] + [saved.at[tick] for tick in range(1, ticks)]
+    outs = [x0, stored[0], s0] + list(stored[1:])
+    targets = [lanes_f[0], lanes_b[0], lanes_b[0]] + [lanes_b[tick] for tick in range(1, ticks)]
+    gates = [None, None, gate_lanes_b[0]] + [None] * (ticks - 1)
+    gathers = [
+        gather_pieces(source, pieces.at[i], send_y.at[i], recv_y.at[i])
+        for i, source in enumerate(sources)
+    ]
+    leaving = []
+    for i, out in enumerate(outs):
+        wait_all(gathers[i])
+        leaving += send_slots(
+            out, buffers.at[i], pieces.at[i], targets[i], gates[i], send_z.at[i], recv_z.at[i]
+        )
+    wait_all(leaving)
+
+
+def section_places(step):
+    count = lax.axis_size("section")
+    return [
+        {"section": ring("section", step % count), "expert": ring("expert", turn)}
+        for turn in range(lax.axis_size("expert"))
+    ]
+
+
+def turn_kernel(
+    tick, targets_f, gates_f, targets_b, lanes_f, lanes_b, gate_lanes_b,
+    partial_f, partial_b, base_f, base_b, fresh_f, fresh_b,
+    out_f, out_b, next_f, next_b, x, s,
+    arrived_f, arrived_b, buffer_f, buffer_b, returned_f, returned_b,
+    fresh, fresh_pieces, pieces, slot_buffers,
+    send_p, recv_p, send_r, recv_r, send_n, recv_n, send_x, recv_x, send_z, recv_z,
+):
+    section, mine = lax.axis_index("section"), lax.axis_index("expert")
+    is_first, is_last = section == 0, section == lax.axis_size("section") - 1
+    greet(peers("expert") + peers("dp") + section_places(1) + section_places(-1))
+    partials, arrived = (partial_f, partial_b), (arrived_f, arrived_b)
+    copies = start_partials(partials, arrived, send_p, recv_p)
+    fresh[...] = jnp.where(is_first, fresh_f[...], fresh_b[...])
+    fresh_copies = gather_pieces(fresh, fresh_pieces, send_n, recv_n)
+    leaving = finish_partials(
+        copies, partials, arrived, (buffer_f, buffer_b), (returned_f, returned_b), send_r, recv_r
+    )
+    wait_all(leaving)
+    shifts = []
+    for stream, (out, step) in enumerate(((out_f, 1), (out_b, -1))):
+        if stream == 0:
+            out[...] = combined(base_f[...], returned_f, targets_f[tick], gates_f[tick])
+        else:
+            out[...] = combined(base_b[...], returned_b, targets_b[tick], None)
+        shifts.append(
+            [
+                remote(
+                    out, pieces.at[stream, mine], send_x.at[stream, turn], recv_x.at[stream, turn],
+                    place,
+                )
+                for turn, place in enumerate(section_places(step))
+            ]
+        )
+    wait_all(fresh_copies)
+    ends, nexts, outs = (is_first, is_last), (next_f, next_b), (x, s)
+    targets = (lanes_f[tick + 1], lanes_b[tick + 1])
+    gates = (None, gate_lanes_b[tick + 1])
+    leaving = []
+    for stream in range(2):
+        wait_all(shifts[stream])
+        for piece in range(fresh_pieces.shape[0]):
+            pieces[stream, piece] = jnp.where(
+                ends[stream], fresh_pieces[piece], pieces[stream, piece]
+            )
+        nexts[stream][...] = pieces[stream, mine]
+        leaving += send_slots(
+            outs[stream], slot_buffers.at[stream], pieces.at[stream], targets[stream],
+            gates[stream], send_z.at[stream], recv_z.at[stream],
+        )
+    wait_all(leaving)
+
+
+def leave_kernel(
+    tick, targets_f, gates_f, targets_b, partial_f, partial_b, base_f, base_b, old_f, old_b,
+    squares, out_f, out_b, total,
+    arrived_f, arrived_b, buffer_f, buffer_b, returned_f, returned_b, sums, landed,
+    send_p, recv_p, send_r, recv_r, send_q, recv_q,
+):
+    greet(peers("section") + peers("expert") + peers("dp"))
+    partials, arrived = (partial_f, partial_b), (arrived_f, arrived_b)
+
+    current, slot = squares, 0
+    for stage, axis in enumerate(("section", "expert", "dp")):
+        others = peers(axis)
+        small = [
+            remote(
+                current, landed.at[slot + turn], send_q.at[slot + turn], recv_q.at[slot + turn],
+                place,
+            )
+            for turn, place in enumerate(others)
+        ]
+        if stage == 0:
+            copies = start_partials(partials, arrived, send_p, recv_p)
+        wait_all(small)
+        value = current[...]
+        for turn in range(len(others)):
+            value += landed[slot + turn]
+        if stage < 2:
+            sums[stage] = value
+            current = sums.at[stage]
+        else:
+            total[...] = value
+        slot += len(others)
+
+    leaving = finish_partials(
+        copies, partials, arrived, (buffer_f, buffer_b), (returned_f, returned_b), send_r, recv_r
+    )
+    wait_all(leaving)
+    for earlier in range(tick):
+        out_f[earlier] = old_f[...]
+        out_b[earlier] = old_b[...]
+    out_f[tick] = combined(base_f[...], returned_f, targets_f[tick], gates_f[tick])
+    out_b[tick] = combined(base_b[...], returned_b, targets_b[tick], None)
+
+
+def talk(kernel, number, shapes, scratch, name):
+    return pl.pallas_call(
+        kernel,
+        out_shape=[jax.ShapeDtypeStruct(*shape) for shape in shapes],
+        scratch_shapes=scratch,
+        compiler_params=pltpu.CompilerParams(
+            vmem_limit_bytes=VMEM_LIMIT, collective_id=number, has_side_effects=True
+        ),
+        name=name,
+    )
 
 
 def put_pieces(out_ref, acc_ref):
@@ -160,9 +388,10 @@
         squares[...] = jnp.full(squares.shape, total, f32)
 
 
-def grad_kernel(factor, xb0, xb1, s0, s1, hid, slope0, slope1, gate_out, down_out):
+def grad_kernel(clip_limit, squares, xb0, xb1, s0, s1, hid, slope0, slope1, gate_out, down_out):
     rows = xb0.shape[0]
-    scale = factor[0]
+    norm = jnp.sqrt(squares[0:1, 0:1])
+    scale = clip_limit / jnp.maximum(norm, clip_limit)
     down_sum = tn(hid[0:rows, :], s0[...]) + tn(hid[rows : 2 * rows, :], s1[...])
     down_out[...] = (down_sum * scale).astype(bf16)
     gate_sum = tn(slope0[...], xb0[...]) + tn(slope1[...], xb1[...])
@@ -172,15 +401,6 @@
 def params():
     return pltpu.CompilerParams(
         dimension_semantics=("arbitrary",), vmem_limit_bytes=VMEM_LIMIT
-    )
-
-
-def plain(kernel, shapes, name):
-    return pl.pallas_call(
-        kernel,
-        out_shape=[jax.ShapeDtypeStruct(s, bf16) for s in shapes],
-        name=name,
-        compiler_params=pltpu.CompilerParams(vmem_limit_bytes=VMEM_LIMIT),
     )
 
 
@@ -207,9 +427,6 @@
     section_count = lax.axis_size("section")
     expert_count = lax.axis_size("dp")
     feature_parts = lax.axis_size("expert")
-    section_index = lax.axis_index("section")
-    is_first = section_index == 0
-    is_last = section_index == section_count - 1
     tick_count, tokens = fwd_experts.shape[1], fwd_experts.shape[2]
     part = fwd_input.shape[-1]
     rows = expert_count * SLOTS
@@ -222,39 +439,45 @@
     lanes_b = jnp.swapaxes(targets_b, 1, 2)
     gate_lanes_b = jnp.swapaxes(bwd_gates[0], 1, 2)
 
-    def over_dp(value):
-        return lax.all_to_all(value, "dp", split_axis=0, concat_axis=0, tiled=True)
-
-    def dispatch(tick, input_part, grad_part):
-        pieces = lax.all_gather(jnp.concatenate([input_part, grad_part], axis=0), "expert", axis=0)
-        x, s = plain(
-            functools.partial(step_dispatch_kernel, tokens),
-            [(rows, width)] * 2,
-            "step_dispatch",
-        )(lanes_f[tick], lanes_b[tick], gate_lanes_b[tick], pieces)
-        return over_dp(x), over_dp(s)
-
-    def collect(tick, partial_f, partial_b, input_part, grad_part):
-        swapped = lax.all_to_all(
-            jnp.concatenate([partial_f, partial_b], axis=1),
-            "expert", split_axis=0, concat_axis=0, tiled=True,
-        )
-        summed = jnp.sum(swapped.astype(f32), axis=0).astype(bf16)
-        r_f, r_b = over_dp(summed[:rows]), over_dp(summed[rows:])
-        return plain(combine_kernel, [(tokens, part)] * 2, "combine")(
-            targets_f[tick], fwd_gates[0, tick], targets_b[tick], r_f, r_b, input_part, grad_part
-        )
-
-    saved_pieces = lax.all_gather(bwd_saved[0].reshape(tick_count * tokens, part), "expert", axis=0)
-    stored = plain(
-        functools.partial(saved_dispatch_kernel, tokens),
-        [(rows, width)] * tick_count,
-        "saved_dispatch",
-    )(lanes_b, saved_pieces)
-    stored0, stored1 = [over_dp(value) for value in stored]
-
+    dma = pltpu.SemaphoreType.DMA
+    others, far = feature_parts - 1, expert_count - 1
+    slot_shape = ((expert_count, SLOTS, width), bf16)
+    part_shape = ((tokens, part), bf16)
+
+    def flat(value):
+        return value.reshape(rows, width)
+
+    def split(value):
+        return value.reshape(feature_parts, expert_count, SLOTS, part)
+
+    def collect_scratch():
+        return [
+            *[pltpu.VMEM((others, expert_count, SLOTS, part), bf16)] * 2,
+            *[pltpu.VMEM((far, SLOTS, part), bf16)] * 2,
+            *[pltpu.VMEM((expert_count, SLOTS, part), bf16)] * 2,
+        ]
+
+    collect_sems = [
+        *[dma((2, others, expert_count))] * 2,
+        *[dma((2, far))] * 2,
+    ]
+    streams = 2 + tick_count
     input_part, grad_part = fwd_input[0], out_grad[0]
-    x0, scaled0 = dispatch(0, input_part, grad_part)
+    x0, scaled0, stored0, stored1 = map(
+        flat,
+        talk(
+            enter_kernel,
+            0,
+            [slot_shape] * streams,
+            [
+                pltpu.VMEM((streams, feature_parts, tokens, part), bf16),
+                pltpu.VMEM((streams, far, SLOTS, width), bf16),
+                *[dma((streams, others))] * 2,
+                *[dma((streams, far))] * 2,
+            ],
+            "enter",
+        )(lanes_f, lanes_b, gate_lanes_b, input_part, grad_part, bwd_saved[0]),
+    )
 
     def unit_block(count):
         return pl.BlockSpec((count, block), lambda i: (0, i))
@@ -288,13 +511,27 @@
         ),
         name="first_step",
     )(x0, stored0, stored1, scaled0, gate_weight, down_weight)
-    produced0, returned0 = collect(0, out_f, out_b, input_part, grad_part)
-
-    arriving = shifted(produced0, "section", 1)
-    leaving = shifted(returned0, "section", -1)
-    input_part = jnp.where(is_first, fresh_input[0], arriving)
-    grad_part = jnp.where(is_last, fresh_grad[0], leaving)
-    x1, scaled1 = dispatch(1, input_part, grad_part)
+    produced0, returned0, input_part, grad_part, x1, scaled1 = talk(
+        functools.partial(turn_kernel, 0),
+        1,
+        [part_shape] * 4 + [slot_shape] * 2,
+        [
+            *collect_scratch(),
+            pltpu.VMEM((tokens, part), bf16),
+            pltpu.VMEM((feature_parts, tokens, part), bf16),
+            pltpu.VMEM((2, feature_parts, tokens, part), bf16),
+            pltpu.VMEM((2, far, SLOTS, width), bf16),
+            *collect_sems,
+            *[dma((others,))] * 2,
+            *[dma((2, feature_parts))] * 2,
+            *[dma((2, far))] * 2,
+        ],
+        "turn",
+    )(
+        targets_f, fwd_gates[0], targets_b, lanes_f, lanes_b, gate_lanes_b,
+        split(out_f), split(out_b), input_part, grad_part, fresh_input[0], fresh_grad[0],
+    )
+    x1, scaled1 = flat(x1), flat(scaled1)
     out_f, out_b, slope1, squares = pl.pallas_call(
         second_step_kernel,
         grid=(steps,),
@@ -322,18 +559,32 @@
         name="second_step",
     )(x1, scaled1, scaled0, stored0, stored1, gate_weight, down_weight, hid, slope0, tilt)
 
-    everyone = lax.all_gather(squares, ("section", "expert", "dp"), axis=0)
-    total = jnp.sum(everyone[:, 0, 0])
     clip_limit = 0.25 * math.sqrt(
         2.0 * section_count * expert_count * feature_parts * hidden_units * width
     )
-    factor = clip_limit / jnp.maximum(jnp.sqrt(total), clip_limit)
-    produced1, returned1 = collect(1, out_f, out_b, input_part, grad_part)
+    small = section_count - 1 + others + far
+    result_shape = ((tick_count, tokens, part), bf16)
+    fwd_output, input_grad, total = talk(
+        functools.partial(leave_kernel, 1),
+        2,
+        [result_shape, result_shape, ((8, 128), f32)],
+        [
+            *collect_scratch(),
+            pltpu.VMEM((2, 8, 128), f32),
+            pltpu.VMEM((small, 8, 128), f32),
+            *collect_sems,
+            *[dma((small,))] * 2,
+        ],
+        "leave",
+    )(
+        targets_f, fwd_gates[0], targets_b, split(out_f), split(out_b), input_part, grad_part,
+        produced0, returned0, squares,
+    )
 
     gate_grad, down_grad = pl.pallas_call(
-        grad_kernel,
+        functools.partial(grad_kernel, clip_limit),
         grid=(steps,),
-        in_specs=[pl.BlockSpec(memory_space=pltpu.SMEM)]
+        in_specs=[whole_spec(total)]
         + [row_spec] * 4
         + [unit_block(2 * rows), unit_block(rows), unit_block(rows)],
         out_specs=[weight_spec] * 2,
@@ -343,11 +594,9 @@
             flops=4 * matmul, bytes_accessed=weight_bytes, transcendentals=0
         ),
         name="weight_grads",
-    )(factor.reshape(1), stored0, stored1, scaled0, scaled1, hid, slope0, slope1)
-
-    fwd_output = jnp.stack([produced0, produced1])[None]
-    input_grad = jnp.stack([returned0, returned1])[None]
-    return (fwd_output, input_grad, gate_grad[None, None], down_grad[None, None])
+    )(total, stored0, stored1, scaled0, scaled1, hid, slope0, slope1)
+
+    return (fwd_output[None], input_grad[None], gate_grad[None, None], down_grad[None, None])
 
 
 def solution(mesh):

time: 389 us -> 248 us (0.64)
  blocking collectives: 244 us -> 0 us
  Pallas kernels: 84.3 us -> 240 us
  starting transfers between devices: 25.6 us -> 0 us
  waiting for transfers between devices: 11.9 us -> 0 us
  other arithmetic: 10.8 us -> 0.39 us
    pallas_call x6 -> x4, Pallas kernels: 32.2 us -> 188 us  [the longest x1 66.3 us: on_device(): talk(enter_kernel, 0, [slot_shape] * streams, [pltpu.VMEM((streams, featu...]
    all_to_all x8 -> x0, blocking collectives: 156 us -> none  [the longest x6 120 us: over_dp(): return lax.all_to_all(value, 'dp', split_axis=0, concat_axis=0, tiled=True)]
    all_gather x4 -> x0, blocking collectives: 88.9 us -> none  [the longest x1 65.5 us: on_device(): everyone = lax.all_gather(squares, ('section', 'expert', 'dp'), axis=0)]
    all_to_all x4 -> x0, starting transfers between devices: 23 us -> none  [over_dp(): return lax.all_to_all(value, 'dp', split_axis=0, concat_axis=0, tiled=True)]
    all_to_all x4 -> x0, waiting for transfers between devices: 8.03 us -> none  [over_dp(): return lax.all_to_all(value, 'dp', split_axis=0, concat_axis=0, tiled=True)]
    squeeze x11 -> x2, local copies, waits for them, and re-layouts: 6.21 us -> 0.16 us  [the longest x1 0.08 us: on_device(): targets_f = slot_targets(fwd_experts[0])]
  transfers between devices with their start and end apart: 6 -> 0, of which waited for: 3 -> 0; matrix products, arithmetic and copies ran while one was open for 1% -> 0% of each run, Pallas kernels for 6% -> 0%
where the time goes in v2:
time: 248 us
  Pallas kernels  240 us (97%)
  local copies, waits for them, and re-layouts  6.1 us (2%)
    pallas_call x1, Pallas kernels, on_device(): talk(enter_kernel, 0, [slot_shape] * streams, [pltpu.VMEM((streams, featu...  66.3 us
    pallas_call x1, Pallas kernels, on_device(): talk(functools.partial(turn_kernel, 0), 1, [part_shape] * 4 + [slot_shape...  59.7 us
    pallas_call x1, Pallas kernels, on_device(): talk(functools.partial(leave_kernel, 1), 2, [result_shape, result_shape,...  41.6 us
    pallas_call x1, Pallas kernels, on_device(): pl.pallas_call(second_step_kernel, grid=(steps,), in_specs=[row_spec] * 5...  27.4 us
    pallas_call x1, Pallas kernels, on_device(): pl.pallas_call(first_step_kernel, grid=(steps,), in_specs=[row_spec] * 4...  24.7 us
    pallas_call x1, Pallas kernels, on_device(): pl.pallas_call(functools.partial(grad_kernel, clip_limit), grid=(steps,),...  20.6 us

profile of v2, /device:TPU:12, one launch (start us, length us, event | category | flops | bytes accessed | tf_op | source)
XLA Modules:
  0.0 247.6 jit_solution(14210145385248661826)
XLA Ops:
  0.6 0.8 copy.22
  1.4 0.1 copy.23
  1.5 0.8 copy.27
  2.3 0.1 copy.28
  2.4 0.4 convert_reduce_fusion
  2.7 0.1 copy.30
  2.9 0.1 copy.25
  3.0 0.0 copy-start
  3.0 0.0 copy-start.1
  3.0 0.7 copy.33.lanes_f
  3.7 0.7 copy.34.lanes_b
  4.3 1.4 copy.26
  5.8 66.3 %enter.1 = (bf16[4,40,2048]{2,1,0:T(8,128)(2,1)}, bf16[4,40,2048]{2,1,0:T(8,128)(2,1)}, bf16[4,40,2048]{2,1,0:T(8,128)(2,1)}, bf16[4,40,2048]{2,1,0:T(8,128)(2,1)}) custom-call(s32[2,2,64]{2,1,0:T(2,128)} %copy.33.lanes_f, s32[2,2,64]{2,1,0:T(2,128)} %copy.34.lanes_b, f32[2,2,64]{2,1,0:T(2,128)} %bitcast.66, bf16[64,1024]{1,0:T(8,128)(2,1)} %bitcast.57, ...), custom_call_target="tpu_custom_call" | custom-call | tf_op jit(solution)/shard_map/enter/pallas_call | solution.py:468
  72.0 24.7 %first_step.1 = (bf16[2,160,1024]{2,1,0:T(8,128)(2,1)}, bf16[2,160,1024]{2,1,0:T(8,128)(2,1)}, bf16[320,3584]{1,0:T(8,128)(2,1)}, bf16[160,3584]{1,0:T(8,128)(2,1)}, f32[160,3584]{1,0:T(8,128)}) custom-call(bf16[160,2048]{1,0:T(8,128)(2,1)} %bitcast.68, bf16[160,2048]{1,0:T(8,128)(2,1)} %bitcast.44, bf16[160,2048]{1,0:T(8,128)(2,1)} %bitcast.47, ...), custom_call_target="tpu_custom_call" | custom-call | flops 14092861440 | bytes 29360128 | tf_op jit(solution)/shard_map/first_step/pallas_call | solution.py:491
  96.8 0.0 copy-done
  96.8 0.0 copy-done.1
  96.8 59.7 %turn.1 = (bf16[64,1024]{1,0:T(8,128)(2,1)}, bf16[64,1024]{1,0:T(8,128)(2,1)}, bf16[64,1024]{1,0:T(8,128)(2,1)}, bf16[64,1024]{1,0:T(8,128)(2,1)}, bf16[4,40,204...) custom-call(s32[2,64,2]{2,1,0:T(8,128)} %copy-done.1, f32[2,64,2]{2,1,0:T(8,128)} %bitcast.53, s32[2,64,2]{2,1,0:T(8,128)} %copy-done, ...), custom_call_target="tpu_custom_call" | custom-call | tf_op jit(solution)/shard_map/turn/pallas_call | solution.py:514
  156.5 27.4 %second_step.1 = (bf16[2,160,1024]{2,1,0:T(8,128)(2,1)}, bf16[2,160,1024]{2,1,0:T(8,128)(2,1)}, bf16[160,3584]{1,0:T(8,128)(2,1)}, f32[8,128]{1,0:T(8,128)}) custom-call(bf16[160,2048]{1,0:T(8,128)(2,1)} %bitcast.52, bf16[160,2048]{1,0:T(8,128)(2,1)} %bitcast.50, bf16[160,2048]{1,0:T(8,128)(2,1)} %bitcast.42, bf16[160,2048]{1,0:T(8,128)(2,1)} %bitcast.45, ...), custom_call_target="tpu_custom_call" | custom-call | flops 9395240960 | bytes 29360128 | tf_op jit(solution)/shard_map/second_step/pallas_call | solution.py:535
  183.9 41.6 %leave.1 = (bf16[2,64,1024]{2,1,0:T(8,128)(2,1)}, bf16[2,64,1024]{2,1,0:T(8,128)(2,1)}, f32[8,128]{1,0:T(8,128)}) custom-call(s32[2,64,2]{2,1,0:T(8,128)} %copy-done.1, f32[2,64,2]{2,1,0:T(8,128)} %bitcast.54, s32[2,64,2]{2,1,0:T(8,128)} %copy-done, bf16[2,4,40,1024]{3,2,1,0:T(8,128)(2,1)} %bitcast.39, bf16[2,4,40,1024]{3,2,1,0:T(8,128)(2,1)} %bitcast.40, ...), custom_call_target="tpu_custom_call" | custom-call | tf_op jit(solution)/shard_map/leave/pallas_call | solution.py:567
  225.6 0.0 copy-start.3
  225.6 0.0 copy-start.2
  225.6 20.6 %weight_grads.1 = (bf16[3584,2048]{1,0:T(8,128)(2,1)}, bf16[3584,2048]{1,0:T(8,128)(2,1)}) custom-call(f32[8,128]{1,0:T(8,128)} %get-tuple-element.48.squares, bf16[160,2048]{1,0:T(8,128)(2,1)} %bitcast.46, bf16[160,2048]{1,0:T(8,128)(2,1)} %bitcast.49, bf16[160,2048]{1,0:T(8,128)(2,1)} %bitcast.43, bf16[160,2048]{1,0:T(8,128)(2,1)} %bitcast.51, ...), custom_call_target="tpu_custom_call" | custom-call | flops 9395240960 | bytes 29360128 | tf_op jit(solution)/shard_map/weight_grads/pallas_call | solution.py:584
  246.2 0.0 copy-done.3
  246.2 0.7 copy.37
  246.9 0.0 copy-done.2
  246.9 0.7 copy.38
  (2 shorter events, 0.0 us)
Async XLA Ops:
  3.0 93.8 %copy-start = (s32[2,64,2]{2,1,0:T(8,128)}, s32[2,64,2]{2,1,0:T(8,128)S(1)}, u32[]{:S(2)}) copy-start(s32[2,64,2]{2,1,0:T(8,128)S(1)} %get-tuple-element.54.targets_b) | copy-start | bytes 3076
  3.0 93.8 %copy-start.1 = (s32[2,64,2]{2,1,0:T(8,128)}, s32[2,64,2]{2,1,0:T(8,128)S(1)}, u32[]{:S(2)}) copy-start(s32[2,64,2]{2,1,0:T(8,128)S(1)} %get-tuple-element.55.targets_f) | copy-start | bytes 3076
  225.6 20.6 %copy-start.3 = (bf16[2,64,1024]{2,1,0:T(8,128)(2,1)S(1)}, bf16[2,64,1024]{2,1,0:T(8,128)(2,1)}, u32[]{:S(2)}) copy-start(bf16[2,64,1024]{2,1,0:T(8,128)(2,1)} %get-tuple-element.46) | copy-start | bytes 786436
  225.6 21.3 %copy-start.2 = (bf16[2,64,1024]{2,1,0:T(8,128)(2,1)S(1)}, bf16[2,64,1024]{2,1,0:T(8,128)(2,1)}, u32[]{:S(2)}) copy-start(bf16[2,64,1024]{2,1,0:T(8,128)(2,1)} %get-tuple-element.47) | copy-start | bytes 786436
